TPU v7x, 8 devices: a whole 2x2x1 slice. The times are simulated.
8 devices in a mesh: rep: 1 (over z), data: 2 (over y), expert: 4 (over x, core).
Axes of the slice: x: 2, y: 2, z: 1, core: 2. Of those that a mesh axis runs over, the one named last changes fastest.
Arguments:
- x: bfloat16 [128, 128, 2304], P(('rep', 'expert', 'data'))
- expert_idx: int32 [128, 128, 2], P(('rep', 'expert', 'data'))
- gate: float32 [128, 128, 2], P(('rep', 'expert', 'data'))
- attn_gain: float32 [2304], replicated
- w_qkv: bfloat16 [2304, 108, 64], P(('data', 'expert'))
- w_out: bfloat16 [36, 64, 2304], P(None, None, ('data', 'expert'))
- moe_gain: float32 [2304], replicated
- w_gate: bfloat16 [8, 2304, 5760], P('expert', 'data')
- w_up: bfloat16 [8, 2304, 5760], P('expert', 'data')
- w_down: bfloat16 [8, 5760, 2304], P('expert', None, 'data')
Outputs:
- output: bfloat16 [128, 128, 2304], P(('rep', 'expert', 'data'))
All inputs are finite; a program needn't handle non-finite values.
Results may differ from a plain program's by a relative error of at most 0.0147271.
Values are sent between devices in bfloat16 or wider.
A program may use at most 1 GiB of HBM per device.

v0:
```python
import functools

import jax
import jax.numpy as jnp
from jax import lax
from jax.experimental import pallas as pl
from jax.experimental.pallas import tpu as pltpu
from jax.sharding import PartitionSpec as P


NORM_EPS = 1e-6
ROPE_BASE = 10000.0


def rms_scale(tok_rows, gain):
    rows_f32 = tok_rows.astype(jnp.float32)
    inv_rms = lax.rsqrt(jnp.mean(rows_f32 * rows_f32, axis=-1, keepdims=True) + NORM_EPS)
    return (rows_f32 * inv_rms * gain).astype(jnp.bfloat16)


def rope_tables(seq_len, head_dim, lanes):
    half_dim = head_dim // 2
    inv_freq = ROPE_BASE ** (-jnp.arange(half_dim, dtype=jnp.float32) * 2.0 / head_dim)
    angles = jnp.arange(seq_len, dtype=jnp.float32)[:, None] * inv_freq[None, :]
    cos_b, sin_b = jnp.cos(angles), jnp.sin(angles)
    times = lanes // head_dim
    return jnp.tile(jnp.concatenate([cos_b, cos_b], axis=1), (1, times)), jnp.tile(jnp.concatenate([-sin_b, sin_b], axis=1), (1, times))


def attention_kernel(head_dim, num_heads, qkv_ref, cos_ref, sin_ref, out_ref):
    seq_len = qkv_ref.shape[0]
    lanes = cos_ref.shape[1]
    per_block = lanes // head_dim
    width = num_heads * head_dim
    lane = lax.broadcasted_iota(jnp.int32, (seq_len, lanes), 1)
    low = lane % head_dim < head_dim // 2
    row_id = lax.broadcasted_iota(jnp.int32, (seq_len, seq_len), 0)
    causal = row_id >= lax.broadcasted_iota(jnp.int32, (seq_len, seq_len), 1)
    causal = jnp.concatenate([causal] * per_block, axis=0)
    cos_b, sin_b = cos_ref[...], sin_ref[...]

    def rope(vals):
        vals = vals.astype(jnp.float32)
        turned = jnp.where(low, pltpu.roll(vals, lanes - head_dim // 2, 1), pltpu.roll(vals, head_dim // 2, 1))
        return vals * cos_b + turned * sin_b

    for start in range(0, width, lanes):
        queries = rope(qkv_ref[:, start:start + lanes])
        keys = rope(qkv_ref[:, width + start:width + start + lanes]).astype(jnp.bfloat16)
        values = qkv_ref[:, 2 * width + start:2 * width + start + lanes]
        stacked = jnp.concatenate([jnp.where(lane // head_dim == h, queries, 0.0) for h in range(per_block)], axis=0).astype(jnp.bfloat16)
        scores = lax.dot_general(stacked, keys, (((1,), (1,)), ((), ())), preferred_element_type=jnp.float32) * (head_dim ** -0.5)
        scores = jnp.where(causal, scores, -1e30)
        weights = jnp.exp(scores - jnp.max(scores, axis=1, keepdims=True))
        probs = (weights / jnp.sum(weights, axis=1, keepdims=True)).astype(jnp.bfloat16)
        mixed = jnp.dot(probs, values, preferred_element_type=jnp.float32)
        out = mixed[:seq_len]
        for h in range(1, per_block):
            out = jnp.where(lane // head_dim == h, mixed[h * seq_len:(h + 1) * seq_len], out)
        out_ref[:, start:start + lanes] = out.astype(out_ref.dtype)


def attention_core(qkv, num_seqs, num_heads, head_dim):
    rows, width = qkv.shape
    seq_len = rows // num_seqs
    lanes = 128
    cos_b, sin_b = rope_tables(seq_len, head_dim, lanes)
    table = pl.BlockSpec((seq_len, lanes), lambda i: (0, 0))
    return pl.pallas_call(
        functools.partial(attention_kernel, head_dim, num_heads),
        grid=(num_seqs,),
        in_specs=[pl.BlockSpec((seq_len, width), lambda i: (i, 0)), table, table],
        out_specs=pl.BlockSpec((seq_len, width // 3), lambda i: (i, 0)),
        out_shape=jax.ShapeDtypeStruct((rows, width // 3), jnp.bfloat16),
        compiler_params=pltpu.CompilerParams(dimension_semantics=("arbitrary",), vmem_limit_bytes=32 * 2**20),
        cost_estimate=pl.CostEstimate(flops=40 * 10**9, bytes_accessed=8 * rows * width // 3, transcendentals=rows * seq_len * num_heads),
        name="attention_core",
    )(qkv, cos_b, sin_b)


def capacity_of(tok_dev, top_k, num_experts):
    return 8 * ((5 * top_k * tok_dev + 32 * num_experts - 1) // (32 * num_experts))


def slots_of(flat_ids, num_experts):
    onehot = (flat_ids[:, None] == jnp.arange(num_experts, dtype=jnp.int32)[None, :]).astype(jnp.int32)
    earlier = jnp.cumsum(onehot, axis=0) - onehot
    return jnp.sum(earlier * onehot, axis=1)


def tile_of(size, most):
    return max(t for t in range(128, most + 1, 128) if size % t == 0)


def up_kernel(ids_ref, z_a, z_b, wg_a, wg_b, wu_a, wu_b, *refs):
    mid_ref = refs[-1]
    ff = mid_ref.shape[1]
    w_a = jnp.concatenate([wg_a[0], wu_a[0]], axis=1)
    w_b = jnp.concatenate([wg_b[0], wu_b[0]], axis=1)
    w = jnp.concatenate([w_a, w_b], axis=0)
    rows = mid_ref.shape[0]
    start = pl.multiple_of(pl.program_id(1) * rows, rows)
    z = jnp.concatenate([z_a[pl.ds(start, rows), :], z_b[pl.ds(start, rows), :]], axis=1)
    acc = jnp.dot(z, w, preferred_element_type=jnp.float32)
    act_gate = acc[:, :ff]
    mid_ref[...] = (act_gate * jax.nn.sigmoid(act_gate) * acc[:, ff:]).astype(mid_ref.dtype)


def expert_up(ids, z, wg_own, wg_got, wu_own, wu_got, mid, first, ff, capacity, peer):
    rows, model_dim = z.shape
    half = model_dim // 2
    size, ff_dim = wg_got.shape[2], wg_own.shape[2]
    tiles, skip = size // ff, first // ff
    own = pl.BlockSpec((1, half, ff), lambda j, i, s: (s[0], 0, skip + j))
    got = pl.BlockSpec((1, half, ff), lambda j, i, s: (0 if wg_got.shape[0] == 1 else 1 - s[0], 0, j))
    once = pl.Buffered(buffer_count=1)
    given = [] if mid is None else [mid]
    return pl.pallas_call(
        up_kernel,
        grid_spec=pltpu.PrefetchScalarGridSpec(
            num_scalar_prefetch=1,
            grid=(tiles, rows // capacity),
            in_specs=[
                pl.BlockSpec((rows, half), lambda j, i, s: (0, s[0]), pipeline_mode=once),
                pl.BlockSpec((rows, half), lambda j, i, s: (0, 1 - s[0]), pipeline_mode=once),
                own, got, own, got,
            ] + [pl.BlockSpec(memory_space=pl.ANY)] * len(given),
            out_specs=pl.BlockSpec((capacity, ff), lambda j, i, s: (2 * i + (1 - s[0] if peer else s[0]), skip + j)),
        ),
        out_shape=jax.ShapeDtypeStruct((2 * rows, ff_dim), jnp.bfloat16),
        input_output_aliases={7: 0} if given else {},
        compiler_params=pltpu.CompilerParams(dimension_semantics=("arbitrary", "arbitrary"), vmem_limit_bytes=48 * 2**20),
        cost_estimate=pl.CostEstimate(flops=4 * rows * model_dim * size, bytes_accessed=2 * (rows * model_dim + 2 * model_dim * size + rows * size), transcendentals=rows * size),
        name="expert_up",
    )(ids, z, z, wg_own, wg_got, wu_own, wu_got, *given)


def down_kernel(ids_ref, mid_ref, *refs):
    out_ref = refs[-1]
    w = [r[0] if len(r.shape) == 3 else r[...] for r in refs[:-1]]
    w = w[0] if len(w) == 1 else jnp.concatenate(w, axis=1)
    out_ref[...] = jnp.dot(mid_ref[...], w, preferred_element_type=jnp.float32).astype(out_ref.dtype)


def expert_down(ids, mid, weights, specs, cols):
    rows, ff_dim = mid.shape
    rb = tile_of(rows, 512)
    return pl.pallas_call(
        down_kernel,
        grid_spec=pltpu.PrefetchScalarGridSpec(
            num_scalar_prefetch=1,
            grid=(rows // rb,),
            in_specs=[pl.BlockSpec((rb, ff_dim), lambda i, s: (i, 0))] + specs,
            out_specs=pl.BlockSpec((rb, cols), lambda i, s: (i, 0)),
        ),
        out_shape=jax.ShapeDtypeStruct((rows, cols), jnp.bfloat16),
        compiler_params=pltpu.CompilerParams(dimension_semantics=("arbitrary",), vmem_limit_bytes=48 * 2**20),
        cost_estimate=pl.CostEstimate(flops=2 * rows * cols * ff_dim, bytes_accessed=2 * (rows * cols + cols * ff_dim + rows * ff_dim), transcendentals=0),
    )(ids, mid, *weights)


def combine_kernel(hid_ref, scale_ref, *refs):
    out_ref = refs[-1]
    half = out_ref.shape[1] // 2
    sides = [hid_ref[:, :half].astype(jnp.float32), hid_ref[:, half:].astype(jnp.float32)]
    mixed = [None, None]
    for k in range(len(refs) // 2):
        early, late = refs[2 * k], refs[2 * k + 1]
        rest = half - early.shape[1]
        own = jnp.concatenate([early[...], late[:, :rest]], axis=1).astype(jnp.float32)
        other = late[:, rest:].astype(jnp.float32)
        gate = scale_ref[:, 2 * k:2 * k + 1]
        flip = scale_ref[:, 2 * k + 1:2 * k + 2] > 0
        for side, value in enumerate((jnp.where(flip, other, own), jnp.where(flip, own, other))):
            term = value * gate
            mixed[side] = term if mixed[side] is None else mixed[side] + term
    out_ref[:, :half] = (sides[0] + mixed[0]).astype(out_ref.dtype)
    out_ref[:, half:] = (sides[1] + mixed[1]).astype(out_ref.dtype)


def combine(hidden, scale, parts):
    rows, model_dim = hidden.shape
    rb = 256
    return pl.pallas_call(
        combine_kernel,
        grid=(rows // rb,),
        in_specs=[pl.BlockSpec((rb, a.shape[1]), lambda i: (i, 0)) for a in (hidden, scale, *parts)],
        out_specs=pl.BlockSpec((rb, model_dim), lambda i: (i, 0)),
        out_shape=jax.ShapeDtypeStruct((rows, model_dim), jnp.bfloat16),
        compiler_params=pltpu.CompilerParams(dimension_semantics=("arbitrary",), vmem_limit_bytes=48 * 2**20),
        cost_estimate=pl.CostEstimate(flops=8 * rows * model_dim, bytes_accessed=8 * rows * model_dim, transcendentals=0),
        name="combine",
    )(hidden, scale, *parts)


def solution(mesh):
    tok_spec = P(('rep', 'expert', 'data'), None, None)
    group_axes = ('data', 'expert')
    token_axes = ('expert', 'data')
    data_size, expert_size = mesh.shape['data'], mesh.shape['expert']
    num_experts = expert_size * data_size
    other_data = [(0, 1), (1, 0)]
    other_chip = [(e, e ^ 2) for e in range(expert_size)]
    other_core = [(e, e ^ 1) for e in range(expert_size)]

    def local_step(x_loc, idx_loc, gate_loc, attn_gain, qkv_part, out_part, moe_gain, gate_part, up_part, down_part):
        num_seqs, seq_len, model_dim = x_loc.shape
        num_heads, head_dim = out_part.shape[0], out_part.shape[1]
        tok_dev = num_seqs * seq_len
        top_k = idx_loc.shape[-1]
        capacity = capacity_of(tok_dev, top_k, num_experts)
        half, ff_dim = gate_part.shape[1:]
        mine = lax.axis_index('data')
        place = lax.axis_index('expert')

        ids = jnp.stack([mine.astype(jnp.int32)])
        theirs = 1 - mine

        def swap(value):
            return lax.ppermute(value, 'data', other_data)

        def cross(value):
            return lax.ppermute(value, 'expert', other_chip)

        def plan(flat_ids):
            slot_pos = slots_of(flat_ids, num_experts)
            kept = slot_pos < capacity
            here = kept & (flat_ids % data_size == mine)
            slot = jnp.where(here, flat_ids // data_size * capacity + slot_pos, expert_size * capacity)
            source = jnp.zeros((expert_size * capacity,), jnp.int32)
            source = source.at[slot].set(jnp.arange(tok_dev * top_k, dtype=jnp.int32) // top_k, mode='drop')
            return kept, slot_pos, source

        flat_ids = idx_loc.reshape(tok_dev * top_k)
        kept, slot_pos, source = plan(flat_ids)
        _, _, peer_source = plan(swap(flat_ids))

        def dispatch(normed, source):
            send = normed.at[source].get(mode='promise_in_bounds')
            return lax.all_to_all(send.reshape(expert_size, capacity, model_dim), 'expert', 0, 0, tiled=True).reshape(-1, model_dim)

        def spread(part, first):
            row = lax.dynamic_update_slice(jnp.zeros((data_size, expert_size) + part.shape, part.dtype), part[None, None], (mine, place, 0, 0))
            along, over, row, first = lax.optimization_barrier((swap(part), cross(part), row, first))
            whole = row
            for row, pieces in ((mine, [part, over]), (1 - mine, [along, cross(along)])):
                for chip, piece in enumerate(pieces):
                    there = place ^ (2 * chip)
                    if piece is not part:
                        whole = lax.dynamic_update_slice(whole, piece[None, None], (row, there, 0, 0))
                    whole = lax.dynamic_update_slice(whole, lax.ppermute(piece, 'expert', other_core)[None, None], (row, there ^ 1, 0, 0))
            return whole.reshape(-1, part.shape[1]), first

        ff = tile_of(ff_dim, 384)
        split = (ff_dim // ff + 1) // 2 * ff
        sends = [lax.dynamic_slice(p, (theirs, 0, first), (1, half, size))[0] for first, size in ((0, split), (split, ff_dim - split)) for p in (gate_part, up_part)]
        normed_x = rms_scale(x_loc, attn_gain).reshape(tok_dev, model_dim)
        out_t = out_part.reshape(num_heads * head_dim, -1).T
        w_qkv, (normed_x, source) = spread(qkv_part.reshape(qkv_part.shape[0], -1), (normed_x, source))
        got = [swap(part)[None] for part in sends]
        got_down = swap(lax.dynamic_index_in_dim(down_part, theirs, 0, keepdims=False))

        qkv = jnp.dot(normed_x, w_qkv, preferred_element_type=jnp.float32).astype(jnp.bfloat16)
        w_out_t, qkv = spread(out_t, qkv)
        attended = attention_core(qkv, num_seqs, num_heads, head_dim)
        attn_proj = lax.dot_general(attended, w_out_t, (((1,), (1,)), ((), ())), preferred_element_type=jnp.float32)
        hidden = (x_loc.reshape(tok_dev, model_dim).astype(jnp.float32) + attn_proj).astype(jnp.bfloat16)

        normed = rms_scale(hidden, moe_gain)
        peer_normed = swap(normed)
        own_rows = dispatch(normed, source)
        peer_rows = dispatch(peer_normed, peer_source)
        mid = None
        for first, wg_got, wu_got in ((0, got[0], got[1]), (split, got[2], got[3])):
            for rows, peer in ((own_rows, False), (peer_rows, True)):
                mid = expert_up(ids, rows, gate_part, wg_got, up_part, wu_got, mid, first, ff, capacity, peer)

        early = half // 256 * 256
        late = 2 * half - early
        once = pl.Buffered(buffer_count=1)
        spec_early = pl.BlockSpec((1, ff_dim, early), lambda i, s: (s[0], 0, 0), pipeline_mode=once)
        spec_rest = pl.BlockSpec((1, ff_dim, half - early), lambda i, s: (s[0], 0, early // (half - early)), pipeline_mode=once)
        spec_got = pl.BlockSpec((ff_dim, half), lambda i, s: (0, 0), pipeline_mode=once)

        def back(cols):
            return lax.all_to_all(cols.reshape(num_experts, capacity, -1), token_axes, 0, 0, tiled=True).reshape(num_experts * capacity, -1)

        outs = expert_down(ids, mid, [down_part], [spec_early], early)
        outs, got_down = lax.optimization_barrier((outs, got_down))
        pieces = [back(outs), back(expert_down(ids, mid, [down_part, got_down], [spec_rest, spec_got], late))]

        pick = jnp.where(kept, flat_ids * capacity + slot_pos, 0).reshape(tok_dev, top_k)
        scale = jnp.where(kept, gate_loc.reshape(tok_dev * top_k), 0.0)
        odd = (flat_ids % data_size).astype(jnp.float32)
        scale = jnp.stack([scale, odd], axis=1).reshape(tok_dev, 2 * top_k)
        parts = [p.at[pick[:, k]].get(mode='promise_in_bounds') for k in range(top_k) for p in pieces]
        return combine(hidden, scale, parts).reshape(num_seqs, seq_len, model_dim)

    in_specs = (tok_spec, tok_spec, tok_spec, P(None), P(group_axes, None, None), P(None, None, group_axes), P(None), P('expert', 'data', None), P('expert', 'data', None), P('expert', None, 'data'))

    return jax.shard_map(local_step, mesh=mesh, in_specs=in_specs, out_specs=tok_spec, check_vma=False)
```

profile of v0, /device:TPU:0, one launch (start us, length us, event | category | flops | bytes accessed | tf_op | source)
XLA Modules:
  0.0 1830.8 jit_solution(14502073144676192850)
XLA Ops:
  0.0 9.4 copy.56
  9.4 6.7 copy.57
  28.9 6.7 copy.60
  35.6 16.5 scatter_custom_fusion
  52.2 5.6 multiply_reduce_fusion
  57.9 11.2 broadcast_in_dim.100
  71.2 9.6 multiply_convert_fusion
  80.9 25.8 %collective-permute-done.2 = bf16[288,6912]{1,0:T(8,128)(2,1)} collective-permute-done((bf16[288,6912]{1,0:T(8,128)(2,1)}, bf16[288,6912]{1,0:T(8,128)(2,1)}, u32[]{:S(2)}, u32[]{:S(2)}) %collective-permute-start.2) | collective-permute-done | bytes 3981344 | tf_op jit(solution)/shard_map/ppermute | solution.py:220
  112.0 4.6 broadcast_in_dim.98
  118.0 4.3 bitcast_dynamic-update-slice_fusion.6
  122.3 4.3 bitcast_dynamic-update-slice_fusion.5
  126.9 94.1 %collective-permute-done.7 = bf16[288,6912]{1,0:T(8,128)(2,1)} collective-permute-done((bf16[288,6912]{1,0:T(8,128)(2,1)}, bf16[288,6912]{1,0:T(8,128)(2,1)}, u32[]{:S(2)}, u32[]{:S(2)}) %collective-permute-start.7) | collective-permute-done | bytes 3981344 | tf_op jit(solution)/shard_map/ppermute | solution.py:223
  221.0 4.3 bitcast_dynamic-update-slice_fusion.4
  225.3 4.3 bitcast_dynamic-update-slice_fusion.3
  231.9 4.8 bitcast_dynamic-update-slice_fusion.1
  238.9 74.5 %convolution_convert_fusion.qkv_ref = bf16[2048,6912]{1,0:T(8,128)(2,1)} fusion(bf16[2048,2304]{1,0:T(8,128)(2,1)S(1)} %bitcast.124, bf16[2304,6912]{1,0:T(8,128)(2,1)} %bitcast.119), kind=kOutput, calls=%fused_computation.8 | convolution fusion | flops 65243971584 | bytes 69599232 | tf_op jit(solution)/shard_map/dot_general | solution.py:263
  315.3 77.4 %attention_core.1 = bf16[2048,2304]{1,0:T(8,128)(2,1)S(1)} custom-call(bf16[2048,6912]{1,0:T(8,128)(2,1)} %convolution_convert_fusion.qkv_ref, f32[128,128]{1,0:T(8,128)S(1)} %copy.65.cos_ref, f32[128,128]{1,0:T(8,128)S(1)} %copy.66.sin_ref), custom_call_target="tpu_custom_call" | custom-call | flops 40000000000 | bytes 37748736 | tf_op jit(solution)/shard_map/attention_core/pallas_call | solution.py:69
  392.8 3.7 copy-done.1
  409.1 30.3 %fusion = (f32[2048]{0:T(1024)S(1)}, bf16[2048,2304]{1,0:T(8,128)(2,1)}) fusion(bf16[2048,2304]{1,0:T(8,128)(2,1)} %copy-done.1, bf16[2304,2304]{1,0:T(8,128)(2,1)} %bitcast.28, bf16[16,128,2304]{2,1,0:T(8,128)(2,1)} %param.10), kind=kOutput, calls=%fused_computation.11 | convolution fusion | flops 21771581440 | bytes 38936576 | tf_op jit(solution)/shard_map/dot_general | solution.py:266
  439.5 9.6 fusion.2
  449.5 27.5 %gather_fusion.1 = bf16[2560,2304]{1,0:T(8,128)(2,1)} fusion(bf16[2048,2304]{1,0:T(8,128)(2,1)} %fusion.2, s32[3072]{0:T(1024)S(1)} %pad_clamp_fusion), kind=kCustom, calls=%fused_computation.1 | custom fusion | bytes 23603200 | tf_op jit(solution)/shard_map/gather | solution.py:239
  477.0 6.6 all-to-all-start.1
  483.6 6.4 dynamic-slice_bitcast_fusion.2
  491.8 6.5 dynamic-slice_bitcast_fusion.1
  500.3 5.8 dynamic-slice_bitcast_fusion.4
  506.3 452.5 %collective-permute-done.15 = s32[4096]{0:T(1024)S(1)} collective-permute-done((s32[4096]{0:T(1024)S(1)}, s32[4096]{0:T(1024)S(1)}, u32[]{:S(2)}, u32[]{:S(2)}) %collective-permute-start.15) | collective-permute-done | bytes 16416 | tf_op jit(solution)/shard_map/ppermute | solution.py:220
  961.9 15.7 scatter_custom_fusion.1
  977.7 27.4 %gather_fusion = bf16[2560,2304]{1,0:T(8,128)(2,1)} fusion(bf16[2048,2304]{1,0:T(8,128)(2,1)} %collective-permute-done.14, s32[3072]{0:T(1024)S(1)} %pad_clamp_fusion.1), kind=kCustom, calls=%fused_computation | custom fusion | bytes 23603200 | tf_op jit(solution)/shard_map/gather | solution.py:239
  1005.1 6.3 all-to-all-start
  1011.5 5.9 dynamic-slice_bitcast_fusion.3
  1017.7 10.9 dynamic-slice_bitcast_fusion
  1030.2 87.2 %expert_up.4.refs_0_ = bf16[5120,5760]{1,0:T(8,128)(2,1)} custom-call(s32[1]{0:T(128)} %bitcast.29.ids_ref, bf16[2560,2304]{1,0:T(8,128)(2,1)} %bitcast.39.z_a.z_b, bf16[2560,2304]{1,0:T(8,128)(2,1)} %bitcast.39.z_a.z_b, bf16[2,1152,5760]{2,1,0:T(8,128)(2,1)} %wg_a.7, bf16[1,1152,3072]{2,1,0:T(8,128)(2,1)} %bitcast.41.wg_b, bf16[2,1152,5760]{2,1,0:T(8,128)(2,1)} %wu_a.7, ...), custom_call_target="tpu_custom_call" | custom-call | flops 72477573120 | bytes 55836672 | tf_op jit(solution)/shard_map/expert_up/pallas_call | solution.py:118
  1117.4 23.7 %all-to-all-done = bf16[4,640,2304]{2,1,0:T(8,128)(2,1)} async-done(((bf16[4,640,2304]{2,1,0:T(8,128)(2,1)}), bf16[4,640,2304]{2,1,0:T(8,128)(2,1)}, u32[]{:S(2)}, u32[]{:S(2)}) %all-to-all-start) | async-done | bytes 11796512 | tf_op jit(solution)/shard_map/all_to_all | solution.py:240
  1141.1 87.2 %expert_up.5.refs_0_ = bf16[5120,5760]{1,0:T(8,128)(2,1)} custom-call(s32[1]{0:T(128)} %bitcast.29.ids_ref, bf16[2560,2304]{1,0:T(8,128)(2,1)} %bitcast.33.z_a.z_b, bf16[2560,2304]{1,0:T(8,128)(2,1)} %bitcast.33.z_a.z_b, bf16[2,1152,5760]{2,1,0:T(8,128)(2,1)} %wg_a.7, bf16[1,1152,3072]{2,1,0:T(8,128)(2,1)} %bitcast.41.wg_b, ...), custom_call_target="tpu_custom_call", output_to_operand_aliasing={{}: (7, {})} | custom-call | flops 72477573120 | bytes 55836672 | tf_op jit(solution)/shard_map/expert_up/pallas_call | solution.py:118
  1228.3 77.2 %expert_up.6.refs_0_ = bf16[5120,5760]{1,0:T(8,128)(2,1)} custom-call(s32[1]{0:T(128)} %bitcast.29.ids_ref, bf16[2560,2304]{1,0:T(8,128)(2,1)} %bitcast.39.z_a.z_b, bf16[2560,2304]{1,0:T(8,128)(2,1)} %bitcast.39.z_a.z_b, bf16[2,1152,5760]{2,1,0:T(8,128)(2,1)} %wg_a.7, bf16[1,1152,2688]{2,1,0:T(8,128)(2,1)} %bitcast.35.wg_b, ...), custom_call_target="tpu_custom_call", output_to_operand_aliasing={{}: (7, {})} | custom-call | flops 63417876480 | bytes 50331648 | tf_op jit(solution)/shard_map/expert_up/pallas_call | solution.py:118
  1305.6 77.2 %expert_up.7.mid_ref = bf16[5120,5760]{1,0:T(8,128)(2,1)} custom-call(s32[1]{0:T(128)} %bitcast.29.ids_ref, bf16[2560,2304]{1,0:T(8,128)(2,1)} %bitcast.33.z_a.z_b, bf16[2560,2304]{1,0:T(8,128)(2,1)} %bitcast.33.z_a.z_b, bf16[2,1152,5760]{2,1,0:T(8,128)(2,1)} %wg_a.7, bf16[1,1152,2688]{2,1,0:T(8,128)(2,1)} %bitcast.35.wg_b, ...), custom_call_target="tpu_custom_call", output_to_operand_aliasing={{}: (7, {})} | custom-call | flops 63417876480 | bytes 50331648 | tf_op jit(solution)/shard_map/expert_up/pallas_call | solution.py:118
  1382.8 71.0 %shard_map.100 = bf16[5120,1024]{1,0:T(8,128)(2,1)} custom-call(s32[1]{0:T(128)} %bitcast.29.ids_ref, bf16[5120,5760]{1,0:T(8,128)(2,1)} %expert_up.7.mid_ref, bf16[2,5760,1152]{2,1,0:T(8,128)(2,1)} %refs_0_.3), custom_call_target="tpu_custom_call" | custom-call | flops 60397977600 | bytes 81264640 | tf_op jit(solution)/shard_map/pallas_call | solution.py:148
  1453.7 54.1 %collective-permute-done.20.refs_1_ = bf16[5760,1152]{1,0:T(8,128)(2,1)} collective-permute-done((bf16[5760,1152]{1,0:T(8,128)(2,1)}, bf16[5760,1152]{1,0:T(8,128)(2,1)}, u32[]{:S(2)}, u32[]{:S(2)}) %collective-permute-start.20) | collective-permute-done | bytes 13271072 | tf_op jit(solution)/shard_map/ppermute | solution.py:220
  1507.9 4.1 all-to-all-start.2
  1512.0 87.5 %shard_map.101 = bf16[5120,1280]{1,0:T(8,128)(2,1)} custom-call(s32[1]{0:T(128)} %bitcast.29.ids_ref, bf16[5120,5760]{1,0:T(8,128)(2,1)} %expert_up.7.mid_ref, bf16[2,5760,1152]{2,1,0:T(8,128)(2,1)} %refs_0_.3, bf16[5760,1152]{1,0:T(8,128)(2,1)} %collective-permute-done.20.refs_1_), custom_call_target="tpu_custom_call" | custom-call | flops 75497472000 | bytes 86835200 | tf_op jit(solution)/shard_map/pallas_call | solution.py:148
  1599.5 28.1 %all-to-all-done.2 = bf16[8,640,1024]{2,1,0:T(8,128)(2,1)} async-done(((bf16[8,640,1024]{2,1,0:T(8,128)(2,1)}), bf16[8,640,1024]{2,1,0:T(8,128)(2,1)}, u32[]{:S(2)}, u32[]{:S(2)}) %all-to-all-start.2) | async-done | bytes 10485792 | tf_op jit(solution)/shard_map/all_to_all | solution.py:286
  1627.6 4.3 all-to-all-start.3
  1640.0 16.4 gather_fusion.4
  1656.4 16.3 gather_fusion.2
  1672.6 103.0 %all-to-all-done.3 = bf16[8,640,1280]{2,1,0:T(8,128)(2,1)} async-done(((bf16[8,640,1280]{2,1,0:T(8,128)(2,1)}), bf16[8,640,1280]{2,1,0:T(8,128)(2,1)}, u32[]{:S(2)}, u32[]{:S(2)}) %all-to-all-start.3) | async-done | bytes 13107232 | tf_op jit(solution)/shard_map/all_to_all | solution.py:286
  1775.6 18.5 %gather_fusion.5 = bf16[2048,1280]{1,0:T(8,128)(2,1)} fusion(bf16[5120,1280]{1,0:T(8,128)(2,1)} %bitcast.49, s32[2048]{0:T(1024)S(1)} %get-tuple-element.38), kind=kCustom, calls=%fused_computation.5 | custom fusion | bytes 10493952 | tf_op jit(solution)/shard_map/gather | solution.py:296
  1794.1 18.5 %gather_fusion.3 = bf16[2048,1280]{1,0:T(8,128)(2,1)} fusion(bf16[5120,1280]{1,0:T(8,128)(2,1)} %bitcast.49, s32[2048]{0:T(1024)S(1)} %get-tuple-element.39), kind=kCustom, calls=%fused_computation.3 | custom fusion | bytes 10493952 | tf_op jit(solution)/shard_map/gather | solution.py:296
  1814.8 15.8 combine.1
  (136 shorter events, 60.8 us)
Async XLA Ops:
  0.0 21.0 %copy-start.3 = (bf16[36,64,288]{2,1,0:T(8,128)(2,1)S(1)}, bf16[36,64,288]{2,1,0:T(8,128)(2,1)}, u32[]{:S(2)}) copy-start(bf16[36,64,288]{2,1,0:T(8,128)(2,1)} %param.15) | copy-start | bytes 3981316
  0.0 23.1 %copy-start.9 = (s32[16,128,2]{1,2,0:T(2,128)S(1)}, s32[16,128,2]{1,2,0:T(2,128)}, u32[]{:S(2)}) copy-start(s32[16,128,2]{1,2,0:T(2,128)} %param.11) | copy-start | bytes 49156
  16.1 90.5 %collective-permute-start.2 = (bf16[288,6912]{1,0:T(8,128)(2,1)}, bf16[288,6912]{1,0:T(8,128)(2,1)}, u32[]{:S(2)}, u32[]{:S(2)}) collective-permute-start(bf16[288,6912]{1,0:T(8,128)(2,1)} %copy.57), channel_id=1, source_target_pairs={{0,4},{4,0},{1,5},{5,1},{2,6},{6,2},{3,7},{7,3}} | collective-permute-start | bytes 11943944 | tf_op jit(solution)/shard_map/ppermute | solution.py:220
  19.5 89.2 %collective-permute-start.3 = (bf16[288,6912]{1,0:T(8,128)(2,1)}, bf16[288,6912]{1,0:T(8,128)(2,1)}, u32[]{:S(2)}, u32[]{:S(2)}) collective-permute-start(bf16[288,6912]{1,0:T(8,128)(2,1)} %copy.57), channel_id=1, source_target_pairs={{0,2},{1,3},{2,0},{3,1},{4,6},{5,7},{6,4},{7,5}} | collective-permute-start | bytes 11943944 | tf_op jit(solution)/shard_map/ppermute | solution.py:223
  21.0 96.9 %collective-permute-start.4 = (bf16[288,6912]{1,0:T(8,128)(2,1)}, bf16[288,6912]{1,0:T(8,128)(2,1)}, u32[]{:S(2)}, u32[]{:S(2)}) collective-permute-start(bf16[288,6912]{1,0:T(8,128)(2,1)} %copy.57), channel_id=1, source_target_pairs={{0,1},{1,0},{2,3},{3,2},{4,5},{5,4},{6,7},{7,6}} | collective-permute-start | bytes 11943944 | tf_op jit(solution)/shard_map/ppermute | solution.py:251
  22.6 290.9 %collective-permute-start = (bf16[288,2304]{1,0:T(8,128)(2,1)}, bf16[288,2304]{1,0:T(8,128)(2,1)}, u32[]{:S(2)}, u32[]{:S(2)}) collective-permute-start(bf16[288,2304]{1,0:T(8,128)(2,1)} %copy.53), channel_id=1, source_target_pairs={{0,4},{4,0},{1,5},{5,1},{2,6},{6,2},{3,7},{7,3}} | collective-permute-start | bytes 3981320 | tf_op jit(solution)/shard_map/ppermute | solution.py:220
  23.1 290.4 %collective-permute-start.1 = (bf16[288,2304]{1,0:T(8,128)(2,1)}, bf16[288,2304]{1,0:T(8,128)(2,1)}, u32[]{:S(2)}, u32[]{:S(2)}) collective-permute-start(bf16[288,2304]{1,0:T(8,128)(2,1)} %copy.53), channel_id=1, source_target_pairs={{0,2},{1,3},{2,0},{3,1},{4,6},{5,7},{6,4},{7,5}} | collective-permute-start | bytes 3981320 | tf_op jit(solution)/shard_map/ppermute | solution.py:223
  24.4 44.7 %copy-start.7 = (s32[4096]{0:T(1024)}, s32[4096]{0:T(1024)S(1)}, u32[]{:S(2)}) copy-start(s32[4096]{0:T(1024)S(1)} %eq.71) | copy-start | bytes 49156
  28.1 41.0 %copy-start.5 = (s32[4096]{0:T(1024)}, s32[4096]{0:T(1024)S(1)}, u32[]{:S(2)}) copy-start(s32[4096]{0:T(1024)S(1)} %fusion.11) | copy-start | bytes 49156
  28.9 23.2 %copy-start.14 = (s32[4096]{0:T(1024)}, s32[4096]{0:T(1024)S(1)}, u32[]{:S(2)}) copy-start(s32[4096]{0:T(1024)S(1)} %add_select_fusion.3) | copy-start | bytes 49156
  57.9 11.2 copy-start.2
  57.9 13.3 copy-start.15
  108.7 18.0 collective-permute-start.5
  108.7 112.3 %collective-permute-start.7 = (bf16[288,6912]{1,0:T(8,128)(2,1)}, bf16[288,6912]{1,0:T(8,128)(2,1)}, u32[]{:S(2)}, u32[]{:S(2)}) collective-permute-start(bf16[288,6912]{1,0:T(8,128)(2,1)} %collective-permute-done.2), channel_id=1, source_target_pairs={{0,2},{1,3},{2,0},{3,1},{4,6},{5,7},{6,4},{7,5}} | collective-permute-start | bytes 11943944 | tf_op jit(solution)/shard_map/ppermute | solution.py:223
  111.8 4.9 copy-start.4
  117.8 111.8 %collective-permute-start.6 = (bf16[288,6912]{1,0:T(8,128)(2,1)}, bf16[288,6912]{1,0:T(8,128)(2,1)S(1)}, u32[]{:S(2)}, u32[]{:S(2)}) collective-permute-start(bf16[288,6912]{1,0:T(8,128)(2,1)} %collective-permute-done.2), channel_id=1, source_target_pairs={{0,1},{1,0},{2,3},{3,2},{4,5},{5,4},{6,7},{7,6}} | collective-permute-start | bytes 11943944 | tf_op jit(solution)/shard_map/ppermute | solution.py:251
  126.6 269.9 %collective-permute-start.9 = (bf16[288,2304]{1,0:T(8,128)(2,1)}, bf16[288,2304]{1,0:T(8,128)(2,1)}, u32[]{:S(2)}, u32[]{:S(2)}) collective-permute-start(bf16[288,2304]{1,0:T(8,128)(2,1)} %copy.53), channel_id=1, source_target_pairs={{0,1},{1,0},{2,3},{3,2},{4,5},{5,4},{6,7},{7,6}} | collective-permute-start | bytes 3981320 | tf_op jit(solution)/shard_map/ppermute | solution.py:251
  221.0 15.7 collective-permute-start.8
  229.6 9.3 slice-start
  231.9 7.1 slice-start.1
  236.7 2.3 slice-start.2
  313.4 92.2 %collective-permute-start.11 = (bf16[288,2304]{1,0:T(8,128)(2,1)}, bf16[288,2304]{1,0:T(8,128)(2,1)S(1)}, u32[]{:S(2)}, u32[]{:S(2)}) collective-permute-start(bf16[288,2304]{1,0:T(8,128)(2,1)} %collective-permute-done), channel_id=1, source_target_pairs={{0,1},{1,0},{2,3},{3,2},{4,5},{5,4},{6,7},{7,6}} | collective-permute-start | bytes 3981320 | tf_op jit(solution)/shard_map/ppermute | solution.py:251
  314.0 87.4 %collective-permute-start.12 = (bf16[288,2304]{1,0:T(8,128)(2,1)}, bf16[288,2304]{1,0:T(8,128)(2,1)S(1)}, u32[]{:S(2)}, u32[]{:S(2)}) collective-permute-start(bf16[288,2304]{1,0:T(8,128)(2,1)} %collective-permute-done), channel_id=1, source_target_pairs={{0,2},{1,3},{2,0},{3,1},{4,6},{5,7},{6,4},{7,5}} | collective-permute-start | bytes 3981320 | tf_op jit(solution)/shard_map/ppermute | solution.py:223
  315.3 86.6 %collective-permute-start.10 = (bf16[288,2304]{1,0:T(8,128)(2,1)}, bf16[288,2304]{1,0:T(8,128)(2,1)S(1)}, u32[]{:S(2)}, u32[]{:S(2)}) collective-permute-start(bf16[288,2304]{1,0:T(8,128)(2,1)} %collective-permute-done.1), channel_id=1, source_target_pairs={{0,1},{1,0},{2,3},{3,2},{4,5},{5,4},{6,7},{7,6}} | collective-permute-start | bytes 3981320 | tf_op jit(solution)/shard_map/ppermute | solution.py:251
  392.8 3.7 copy-start.1
  401.5 6.5 collective-permute-start.13
  409.1 30.4 %copy-start.16 = (f32[2304]{0:T(1024)S(1)}, f32[2304]{0:T(1024)}, u32[]{:S(2)}) copy-start(f32[2304]{0:T(1024)} %param.16) | copy-start | bytes 27652
  439.5 10.0 copy-start.12
  449.1 528.5 %collective-permute-start.14 = (bf16[2048,2304]{1,0:T(8,128)(2,1)}, bf16[2048,2304]{1,0:T(8,128)(2,1)}, u32[]{:S(2)}, u32[]{:S(2)}) collective-permute-start(bf16[2048,2304]{1,0:T(8,128)(2,1)} %fusion.2), channel_id=1, source_target_pairs={{0,4},{4,0},{1,5},{5,1},{2,6},{6,2},{3,7},{7,3}} | collective-permute-start | bytes 28311560 | tf_op jit(solution)/shard_map/ppermute | solution.py:220
  477.0 528.2 %all-to-all-start.1 = ((bf16[4,640,2304]{2,1,0:T(8,128)(2,1)}), bf16[4,640,2304]{2,1,0:T(8,128)(2,1)}, u32[]{:S(2)}, u32[]{:S(2)}) async-start(bf16[4,640,2304]{2,1,0:T(8,128)(2,1)} %bitcast.117), calls=%async_computation.1 | async-start | bytes 23592960 | tf_op jit(solution)/shard_map/all_to_all | solution.py:240
  490.0 8.5 copy-start.8
  490.0 540.2 %collective-permute-start.18 = (bf16[1152,3072]{1,0:T(8,128)(2,1)}, bf16[1152,3072]{1,0:T(8,128)(2,1)}, u32[]{:S(2)}, u32[]{:S(2)}) collective-permute-start(bf16[1152,3072]{1,0:T(8,128)(2,1)} %dynamic-slice_bitcast_fusion.2), channel_id=1, source_target_pairs={{0,4},{4,0},{1,5},{5,1},{2,6},{6,2},{3,7},{7,3}} | collective-permute-start | bytes 21233672 | tf_op jit(solution)/shard_map/ppermute | solution.py:220
  498.2 532.0 %collective-permute-start.19 = (bf16[1152,3072]{1,0:T(8,128)(2,1)}, bf16[1152,3072]{1,0:T(8,128)(2,1)}, u32[]{:S(2)}, u32[]{:S(2)}) collective-permute-start(bf16[1152,3072]{1,0:T(8,128)(2,1)} %dynamic-slice_bitcast_fusion.1), channel_id=1, source_target_pairs={{0,4},{4,0},{1,5},{5,1},{2,6},{6,2},{3,7},{7,3}} | collective-permute-start | bytes 21233672 | tf_op jit(solution)/shard_map/ppermute | solution.py:220
  498.5 460.3 %collective-permute-start.15 = (s32[4096]{0:T(1024)S(1)}, s32[4096]{0:T(1024)S(1)}, u32[]{:S(2)}, u32[]{:S(2)}) collective-permute-start(s32[4096]{0:T(1024)S(1)} %copy-done.8), channel_id=1, source_target_pairs={{0,4},{4,0},{1,5},{5,1},{2,6},{6,2},{3,7},{7,3}} | collective-permute-start | bytes 49160 | tf_op jit(solution)/shard_map/ppermute | solution.py:220
  506.1 722.3 %collective-permute-start.16 = (bf16[1152,2688]{1,0:T(8,128)(2,1)}, bf16[1152,2688]{1,0:T(8,128)(2,1)}, u32[]{:S(2)}, u32[]{:S(2)}) collective-permute-start(bf16[1152,2688]{1,0:T(8,128)(2,1)} %dynamic-slice_bitcast_fusion.4), channel_id=1, source_target_pairs={{0,4},{4,0},{1,5},{5,1},{2,6},{6,2},{3,7},{7,3}} | collective-permute-start | bytes 18579464 | tf_op jit(solution)/shard_map/ppermute | solution.py:220
  1005.1 136.0 %all-to-all-start = ((bf16[4,640,2304]{2,1,0:T(8,128)(2,1)}), bf16[4,640,2304]{2,1,0:T(8,128)(2,1)}, u32[]{:S(2)}, u32[]{:S(2)}) async-start(bf16[4,640,2304]{2,1,0:T(8,128)(2,1)} %bitcast.118), calls=%async_computation | async-start | bytes 23592960 | tf_op jit(solution)/shard_map/all_to_all | solution.py:240
  1017.3 211.0 %collective-permute-start.17 = (bf16[1152,2688]{1,0:T(8,128)(2,1)}, bf16[1152,2688]{1,0:T(8,128)(2,1)}, u32[]{:S(2)}, u32[]{:S(2)}) collective-permute-start(bf16[1152,2688]{1,0:T(8,128)(2,1)} %dynamic-slice_bitcast_fusion.3), channel_id=1, source_target_pairs={{0,4},{4,0},{1,5},{5,1},{2,6},{6,2},{3,7},{7,3}} | collective-permute-start | bytes 18579464 | tf_op jit(solution)/shard_map/ppermute | solution.py:220
  1028.5 479.3 %collective-permute-start.20 = (bf16[5760,1152]{1,0:T(8,128)(2,1)}, bf16[5760,1152]{1,0:T(8,128)(2,1)}, u32[]{:S(2)}, u32[]{:S(2)}) collective-permute-start(bf16[5760,1152]{1,0:T(8,128)(2,1)} %dynamic-slice_bitcast_fusion), channel_id=1, source_target_pairs={{0,4},{4,0},{1,5},{5,1},{2,6},{6,2},{3,7},{7,3}} | collective-permute-start | bytes 39813128 | tf_op jit(solution)/shard_map/ppermute | solution.py:220
  1507.9 119.8 %all-to-all-start.2 = ((bf16[8,640,1024]{2,1,0:T(8,128)(2,1)}), bf16[8,640,1024]{2,1,0:T(8,128)(2,1)}, u32[]{:S(2)}, u32[]{:S(2)}) async-start(bf16[8,640,1024]{2,1,0:T(8,128)(2,1)} %bitcast.121), calls=%async_computation.2 | async-start | bytes 20971520 | tf_op jit(solution)/shard_map/all_to_all | solution.py:286
  1627.6 4.3 copy-start.6
  1627.6 6.3 copy-start.10
  1627.6 7.7 copy-start.13
  1627.6 8.8 copy-start.11
  1627.6 148.0 %all-to-all-start.3 = ((bf16[8,640,1280]{2,1,0:T(8,128)(2,1)}), bf16[8,640,1280]{2,1,0:T(8,128)(2,1)}, u32[]{:S(2)}, u32[]{:S(2)}) async-start(bf16[8,640,1280]{2,1,0:T(8,128)(2,1)} %bitcast.120), calls=%async_computation.3 | async-start | bytes 26214400 | tf_op jit(solution)/shard_map/all_to_all | solution.py:286
  1812.6 2.2 copy-start
where the time goes:
time: 1840 us; the launch traced here: 1830 us
  waiting for transfers between devices  783 us (43%)
  Pallas kernels  580 us (32%)
  local copies, waits for them, and re-layouts  290 us (16%)
  matrix products  105 us (6%)
  starting transfers between devices  37.5 us (2%)
  other arithmetic  34 us (2%)
    ppermute x9, waiting for transfers between devices, swap(): return lax.ppermute(value, 'data', other_data)  532 us
    pallas_call x4, Pallas kernels, expert_up(): pl.pallas_call(up_kernel, grid_spec=pltpu.PrefetchScalarGridSpec(num_scal...  329 us
    pallas_call x2, Pallas kernels, expert_down(): pl.pallas_call(down_kernel, grid_spec=pltpu.PrefetchScalarGridSpec(num_sc...  158 us
    all_to_all x2, waiting for transfers between devices, back(): lax.all_to_all(cols.reshape(num_experts, capacity, -1), token_axes, 0, 0,...  131 us
    ppermute x4, waiting for transfers between devices, cross(): return lax.ppermute(value, 'expert', other_chip)  96.2 us
    pallas_call x1, Pallas kernels, attention_core(): pl.pallas_call(functools.partial(attention_kernel, head_dim, num_heads),...  77.4 us
    dot_general x1, matrix products, local_step(): jnp.dot(normed_x, w_qkv, preferred_element_type=jnp.float32)  74.5 us
    gather x4, local copies, waits for them, and re-layouts, local_step(): p.at[pick[:, k]].get(mode='promise_in_bounds')  69.6 us
  transfers between devices with their start and end apart: 25, of which 8 were waited for; matrix products, arithmetic and copies ran while one was open for 18% of the time, Pallas kernels for 31%

commit v1 on v0

--- a/solution.py
+++ b/solution.py
@@ -166,9 +166,8 @@
     mixed = [None, None]
     for k in range(len(refs) // 2):
         early, late = refs[2 * k], refs[2 * k + 1]
-        rest = half - early.shape[1]
-        own = jnp.concatenate([early[...], late[:, :rest]], axis=1).astype(jnp.float32)
-        other = late[:, rest:].astype(jnp.float32)
+        own = early[:, :half].astype(jnp.float32)
+        other = jnp.concatenate([early[:, half:], late[...]], axis=1).astype(jnp.float32)
         gate = scale_ref[:, 2 * k:2 * k + 1]
         flip = scale_ref[:, 2 * k + 1:2 * k + 2] > 0
         for side, value in enumerate((jnp.where(flip, other, own), jnp.where(flip, own, other))):
@@ -256,9 +255,12 @@
         sends = [lax.dynamic_slice(p, (theirs, 0, first), (1, half, size))[0] for first, size in ((0, split), (split, ff_dim - split)) for p in (gate_part, up_part)]
         normed_x = rms_scale(x_loc, attn_gain).reshape(tok_dev, model_dim)
         out_t = out_part.reshape(num_heads * head_dim, -1).T
-        w_qkv, (normed_x, source) = spread(qkv_part.reshape(qkv_part.shape[0], -1), (normed_x, source))
+        qkv_part, out_t = lax.optimization_barrier((qkv_part, out_t))
+        qkv_flat = qkv_part.reshape(qkv_part.shape[0], -1)
+        w_qkv, (normed_x, source) = spread(qkv_flat, (normed_x, source))
         got = [swap(part)[None] for part in sends]
-        got_down = swap(lax.dynamic_index_in_dim(down_part, theirs, 0, keepdims=False))
+        more = half - half // 2 // 256 * 256
+        got_down = [swap(lax.dynamic_slice(down_part, (theirs, 0, first), (1, ff_dim, size))[0]) for first, size in ((0, more), (more, half - more))]
 
         qkv = jnp.dot(normed_x, w_qkv, preferred_element_type=jnp.float32).astype(jnp.bfloat16)
         w_out_t, qkv = spread(out_t, qkv)
@@ -275,19 +277,17 @@
             for rows, peer in ((own_rows, False), (peer_rows, True)):
                 mid = expert_up(ids, rows, gate_part, wg_got, up_part, wu_got, mid, first, ff, capacity, peer)
 
-        early = half // 256 * 256
-        late = 2 * half - early
         once = pl.Buffered(buffer_count=1)
-        spec_early = pl.BlockSpec((1, ff_dim, early), lambda i, s: (s[0], 0, 0), pipeline_mode=once)
-        spec_rest = pl.BlockSpec((1, ff_dim, half - early), lambda i, s: (s[0], 0, early // (half - early)), pipeline_mode=once)
-        spec_got = pl.BlockSpec((ff_dim, half), lambda i, s: (0, 0), pipeline_mode=once)
+        spec_own = pl.BlockSpec((1, ff_dim, half), lambda i, s: (s[0], 0, 0), pipeline_mode=once)
+        spec_got = [pl.BlockSpec(part.shape, lambda i, s: (0, 0), pipeline_mode=once) for part in got_down]
 
         def back(cols):
             return lax.all_to_all(cols.reshape(num_experts, capacity, -1), token_axes, 0, 0, tiled=True).reshape(num_experts * capacity, -1)
 
-        outs = expert_down(ids, mid, [down_part], [spec_early], early)
-        outs, got_down = lax.optimization_barrier((outs, got_down))
-        pieces = [back(outs), back(expert_down(ids, mid, [down_part, got_down], [spec_rest, spec_got], late))]
+        outs = expert_down(ids, mid, [down_part, got_down[0]], [spec_own, spec_got[0]], half + more)
+        outs, last_down = lax.optimization_barrier((outs, got_down[1]))
+        last_outs = expert_down(ids, mid, [last_down], [spec_got[1]], half - more)
+        pieces = [back(outs), back(last_outs)]
 
         pick = jnp.where(kept, flat_ids * capacity + slot_pos, 0).reshape(tok_dev, top_k)
         scale = jnp.where(kept, gate_loc.reshape(tok_dev * top_k), 0.0)

time: 1840 us -> 1880 us (1.022)
  blocking collectives: 0 us -> 61.4 us
    all_to_all x0 -> x1, blocking collectives: none -> 61.4 us  [back(): lax.all_to_all(cols.reshape(num_experts, capacity, -1), token_axes, 0, 0,...]
    ppermute x9 -> x10, waiting for transfers between devices: 532 us -> 483 us  [swap(): return lax.ppermute(value, 'data', other_data)]
    all_to_all x2 -> x1, waiting for transfers between devices: 131 us -> 169 us  [back(): lax.all_to_all(cols.reshape(num_experts, capacity, -1), token_axes, 0, 0,...]
  transfers between devices with their start and end apart: 25 -> 25, of which waited for: 8 -> 7; matrix products, arithmetic and copies ran while one was open for 18% -> 17% of each run, Pallas kernels for 31% -> 28%
where the time goes in v1:
time: 1880 us
  waiting for transfers between devices  770 us (41%)
  Pallas kernels  580 us (31%)
  local copies, waits for them, and re-layouts  291 us (15%)
  matrix products  105 us (6%)
  blocking collectives  61.4 us (3%)
  starting transfers between devices  34.4 us (2%)
  other arithmetic  34 us (2%)
    ppermute x10, waiting for transfers between devices, swap(): return lax.ppermute(value, 'data', other_data)  483 us
    pallas_call x4, Pallas kernels, expert_up(): pl.pallas_call(up_kernel, grid_spec=pltpu.PrefetchScalarGridSpec(num_scal...  329 us
    all_to_all x1, waiting for transfers between devices, back(): lax.all_to_all(cols.reshape(num_experts, capacity, -1), token_axes, 0, 0,...  169 us
    pallas_call x2, Pallas kernels, expert_down(): pl.pallas_call(down_kernel, grid_spec=pltpu.PrefetchScalarGridSpec(num_sc...  158 us
    ppermute x4, waiting for transfers between devices, cross(): return lax.ppermute(value, 'expert', other_chip)  96.2 us
    pallas_call x1, Pallas kernels, attention_core(): pl.pallas_call(functools.partial(attention_kernel, head_dim, num_heads),...  77.4 us
    dot_general x1, matrix products, local_step(): jnp.dot(normed_x, w_qkv, preferred_element_type=jnp.float32)  74.6 us
    gather x4, local copies, waits for them, and re-layouts, local_step(): p.at[pick[:, k]].get(mode='promise_in_bounds')  69.6 us
  transfers between devices with their start and end apart: 25, of which 7 were waited for; matrix products, arithmetic and copies ran while one was open for 17% of the time, Pallas kernels for 28%

profile of v1, /device:TPU:0, one launch (start us, length us, event | category | flops | bytes accessed | tf_op | source)
XLA Modules:
  0.0 1875.4 jit_solution(4970614908859059371)
XLA Ops:
  0.0 9.4 copy.56
  9.4 6.7 copy.57
  28.9 6.7 copy.60
  35.6 16.5 scatter_custom_fusion
  52.2 5.6 multiply_reduce_fusion
  57.9 11.2 broadcast_in_dim.100
  71.2 9.6 multiply_convert_fusion
  80.9 25.7 %collective-permute-done.2 = bf16[288,6912]{1,0:T(8,128)(2,1)} collective-permute-done((bf16[288,6912]{1,0:T(8,128)(2,1)}, bf16[288,6912]{1,0:T(8,128)(2,1)}, u32[]{:S(2)}, u32[]{:S(2)}) %collective-permute-start.2) | collective-permute-done | bytes 3981344 | tf_op jit(solution)/shard_map/ppermute | solution.py:219
  112.0 4.6 broadcast_in_dim.98
  118.0 4.3 bitcast_dynamic-update-slice_fusion.6
  122.3 4.3 bitcast_dynamic-update-slice_fusion.5
  126.8 94.2 %collective-permute-done.7 = bf16[288,6912]{1,0:T(8,128)(2,1)} collective-permute-done((bf16[288,6912]{1,0:T(8,128)(2,1)}, bf16[288,6912]{1,0:T(8,128)(2,1)}, u32[]{:S(2)}, u32[]{:S(2)}) %collective-permute-start.7) | collective-permute-done | bytes 3981344 | tf_op jit(solution)/shard_map/ppermute | solution.py:222
  221.0 4.3 bitcast_dynamic-update-slice_fusion.4
  225.3 4.3 bitcast_dynamic-update-slice_fusion.3
  231.9 4.8 bitcast_dynamic-update-slice_fusion.1
  238.9 74.6 %convolution_convert_fusion.qkv_ref = bf16[2048,6912]{1,0:T(8,128)(2,1)} fusion(bf16[2048,2304]{1,0:T(8,128)(2,1)S(1)} %bitcast.127, bf16[2304,6912]{1,0:T(8,128)(2,1)} %bitcast.123), kind=kOutput, calls=%fused_computation.8 | convolution fusion | flops 65243971584 | bytes 69599232 | tf_op jit(solution)/shard_map/dot_general | solution.py:265
  315.4 77.4 %attention_core.1 = bf16[2048,2304]{1,0:T(8,128)(2,1)S(1)} custom-call(bf16[2048,6912]{1,0:T(8,128)(2,1)} %convolution_convert_fusion.qkv_ref, f32[128,128]{1,0:T(8,128)S(1)} %copy.65.cos_ref, f32[128,128]{1,0:T(8,128)S(1)} %copy.66.sin_ref), custom_call_target="tpu_custom_call" | custom-call | flops 40000000000 | bytes 37748736 | tf_op jit(solution)/shard_map/attention_core/pallas_call | solution.py:69
  392.9 3.7 copy-done.1
  409.2 30.3 %fusion = (f32[2048]{0:T(1024)S(1)}, bf16[2048,2304]{1,0:T(8,128)(2,1)}) fusion(bf16[2048,2304]{1,0:T(8,128)(2,1)} %copy-done.1, bf16[2304,2304]{1,0:T(8,128)(2,1)} %bitcast.27, bf16[16,128,2304]{2,1,0:T(8,128)(2,1)} %param.10), kind=kOutput, calls=%fused_computation.11 | convolution fusion | flops 21771581440 | bytes 38936576 | tf_op jit(solution)/shard_map/dot_general | solution.py:268
  439.5 9.6 fusion.2
  449.5 27.5 %gather_fusion.1 = bf16[2560,2304]{1,0:T(8,128)(2,1)} fusion(bf16[2048,2304]{1,0:T(8,128)(2,1)} %fusion.2, s32[3072]{0:T(1024)S(1)} %pad_clamp_fusion), kind=kCustom, calls=%fused_computation.1 | custom fusion | bytes 23603200 | tf_op jit(solution)/shard_map/gather | solution.py:238
  477.0 6.6 all-to-all-start.1
  483.6 6.4 dynamic-slice_bitcast_fusion.2
  491.7 6.5 dynamic-slice_bitcast_fusion.1
  500.2 5.7 dynamic-slice_bitcast_fusion.4
  506.2 452.6 %collective-permute-done.15 = s32[4096]{0:T(1024)S(1)} collective-permute-done((s32[4096]{0:T(1024)S(1)}, s32[4096]{0:T(1024)S(1)}, u32[]{:S(2)}, u32[]{:S(2)}) %collective-permute-start.15) | collective-permute-done | bytes 16416 | tf_op jit(solution)/shard_map/ppermute | solution.py:219
  962.0 15.7 scatter_custom_fusion.1
  977.7 27.4 %gather_fusion = bf16[2560,2304]{1,0:T(8,128)(2,1)} fusion(bf16[2048,2304]{1,0:T(8,128)(2,1)} %collective-permute-done.14, s32[3072]{0:T(1024)S(1)} %pad_clamp_fusion.1), kind=kCustom, calls=%fused_computation | custom fusion | bytes 23603200 | tf_op jit(solution)/shard_map/gather | solution.py:238
  1005.1 6.4 all-to-all-start
  1011.5 5.8 dynamic-slice_bitcast_fusion.3
  1017.7 6.8 dynamic-slice_bitcast_fusion
  1026.2 5.6 dynamic-slice_bitcast_fusion.5
  1032.1 87.2 %expert_up.4.refs_0_ = bf16[5120,5760]{1,0:T(8,128)(2,1)} custom-call(s32[1]{0:T(128)} %bitcast.28.ids_ref, bf16[2560,2304]{1,0:T(8,128)(2,1)} %bitcast.38.z_a.z_b, bf16[2560,2304]{1,0:T(8,128)(2,1)} %bitcast.38.z_a.z_b, bf16[2,1152,5760]{2,1,0:T(8,128)(2,1)} %wg_a.7, bf16[1,1152,3072]{2,1,0:T(8,128)(2,1)} %bitcast.40.wg_b, bf16[2,1152,5760]{2,1,0:T(8,128)(2,1)} %wu_a.7, ...), custom_call_target="tpu_custom_call" | custom-call | flops 72477573120 | bytes 55836672 | tf_op jit(solution)/shard_map/expert_up/pallas_call | solution.py:118
  1119.3 21.9 %all-to-all-done = bf16[4,640,2304]{2,1,0:T(8,128)(2,1)} async-done(((bf16[4,640,2304]{2,1,0:T(8,128)(2,1)}), bf16[4,640,2304]{2,1,0:T(8,128)(2,1)}, u32[]{:S(2)}, u32[]{:S(2)}) %all-to-all-start) | async-done | bytes 11796512 | tf_op jit(solution)/shard_map/all_to_all | solution.py:239
  1141.2 87.2 %expert_up.5.refs_0_ = bf16[5120,5760]{1,0:T(8,128)(2,1)} custom-call(s32[1]{0:T(128)} %bitcast.28.ids_ref, bf16[2560,2304]{1,0:T(8,128)(2,1)} %bitcast.32.z_a.z_b, bf16[2560,2304]{1,0:T(8,128)(2,1)} %bitcast.32.z_a.z_b, bf16[2,1152,5760]{2,1,0:T(8,128)(2,1)} %wg_a.7, bf16[1,1152,3072]{2,1,0:T(8,128)(2,1)} %bitcast.40.wg_b, ...), custom_call_target="tpu_custom_call", output_to_operand_aliasing={{}: (7, {})} | custom-call | flops 72477573120 | bytes 55836672 | tf_op jit(solution)/shard_map/expert_up/pallas_call | solution.py:118
  1228.4 77.2 %expert_up.6.refs_0_ = bf16[5120,5760]{1,0:T(8,128)(2,1)} custom-call(s32[1]{0:T(128)} %bitcast.28.ids_ref, bf16[2560,2304]{1,0:T(8,128)(2,1)} %bitcast.38.z_a.z_b, bf16[2560,2304]{1,0:T(8,128)(2,1)} %bitcast.38.z_a.z_b, bf16[2,1152,5760]{2,1,0:T(8,128)(2,1)} %wg_a.7, bf16[1,1152,2688]{2,1,0:T(8,128)(2,1)} %bitcast.34.wg_b, ...), custom_call_target="tpu_custom_call", output_to_operand_aliasing={{}: (7, {})} | custom-call | flops 63417876480 | bytes 50331648 | tf_op jit(solution)/shard_map/expert_up/pallas_call | solution.py:118
  1305.6 77.2 %expert_up.7.mid_ref = bf16[5120,5760]{1,0:T(8,128)(2,1)} custom-call(s32[1]{0:T(128)} %bitcast.28.ids_ref, bf16[2560,2304]{1,0:T(8,128)(2,1)} %bitcast.32.z_a.z_b, bf16[2560,2304]{1,0:T(8,128)(2,1)} %bitcast.32.z_a.z_b, bf16[2,1152,5760]{2,1,0:T(8,128)(2,1)} %wg_a.7, bf16[1,1152,2688]{2,1,0:T(8,128)(2,1)} %bitcast.34.wg_b, ...), custom_call_target="tpu_custom_call", output_to_operand_aliasing={{}: (7, {})} | custom-call | flops 63417876480 | bytes 50331648 | tf_op jit(solution)/shard_map/expert_up/pallas_call | solution.py:118
  1382.8 120.6 %shard_map.100 = bf16[5120,1792]{1,0:T(8,128)(2,1)} custom-call(s32[1]{0:T(128)} %bitcast.28.ids_ref, bf16[5120,5760]{1,0:T(8,128)(2,1)} %expert_up.7.mid_ref, bf16[2,5760,1152]{2,1,0:T(8,128)(2,1)} %refs_0_.1, bf16[5760,640]{1,0:T(8,128)(2,1)} %collective-permute-done.20.refs_1_), custom_call_target="tpu_custom_call" | custom-call | flops 105696460800 | bytes 97976320 | tf_op jit(solution)/shard_map/pallas_call | solution.py:148
  1503.3 4.6 collective-permute-done.21.refs_0_
  1507.9 37.2 %shard_map.101 = bf16[5120,512]{1,0:T(8,128)(2,1)S(1)} custom-call(s32[1]{0:T(128)} %bitcast.28.ids_ref, bf16[5120,5760]{1,0:T(8,128)(2,1)} %expert_up.7.mid_ref, bf16[5760,512]{1,0:T(8,128)(2,1)} %collective-permute-done.21.refs_0_), custom_call_target="tpu_custom_call" | custom-call | flops 30198988800 | bytes 70123520 | tf_op jit(solution)/shard_map/pallas_call | solution.py:148
  1545.1 61.4 %all_to_all.20 = bf16[8,640,512]{2,1,0:T(8,128)(2,1)} all-to-all(bf16[8,640,512]{2,1,0:T(8,128)(2,1)S(1)} %bitcast.116), channel_id=1, replica_groups=mesh['rep'=1,'data'=2,'expert'=4] {'expert','data'}, dimensions={0} | all-to-all | bytes 10485760 | tf_op jit(solution)/shard_map/all_to_all | solution.py:285
  1606.6 5.0 all-to-all-start.2
  1619.7 10.8 gather_fusion.5
  1630.4 12.4 gather_fusion.3
  1642.8 168.7 %all-to-all-done.2 = bf16[8,640,1792]{2,1,0:T(8,128)(2,1)} async-done(((bf16[8,640,1792]{2,1,0:T(8,128)(2,1)}), bf16[8,640,1792]{2,1,0:T(8,128)(2,1)}, u32[]{:S(2)}, u32[]{:S(2)}) %all-to-all-start.2) | async-done | bytes 18350112 | tf_op jit(solution)/shard_map/all_to_all | solution.py:285
  1811.5 23.2 %gather_fusion.4 = bf16[2048,1792]{1,0:T(8,128)(2,1)} fusion(bf16[5120,1792]{1,0:T(8,128)(2,1)} %bitcast.46, s32[2048]{0:T(1024)S(1)} %get-tuple-element.42), kind=kCustom, calls=%fused_computation.4 | custom fusion | bytes 14688256 | tf_op jit(solution)/shard_map/gather | solution.py:296
  1834.7 23.2 %gather_fusion.2 = bf16[2048,1792]{1,0:T(8,128)(2,1)} fusion(bf16[5120,1792]{1,0:T(8,128)(2,1)} %bitcast.46, s32[2048]{0:T(1024)S(1)} %get-tuple-element.43), kind=kCustom, calls=%fused_computation.2 | custom fusion | bytes 14688256 | tf_op jit(solution)/shard_map/gather | solution.py:296
  1859.5 15.7 combine.1
  (138 shorter events, 60.5 us)
Async XLA Ops:
  0.0 21.0 %copy-start.3 = (bf16[36,64,288]{2,1,0:T(8,128)(2,1)S(1)}, bf16[36,64,288]{2,1,0:T(8,128)(2,1)}, u32[]{:S(2)}) copy-start(bf16[36,64,288]{2,1,0:T(8,128)(2,1)} %param.15) | copy-start | bytes 3981316
  0.0 23.1 %copy-start.9 = (s32[16,128,2]{1,2,0:T(2,128)S(1)}, s32[16,128,2]{1,2,0:T(2,128)}, u32[]{:S(2)}) copy-start(s32[16,128,2]{1,2,0:T(2,128)} %param.11) | copy-start | bytes 49156
  16.1 90.5 %collective-permute-start.2 = (bf16[288,6912]{1,0:T(8,128)(2,1)}, bf16[288,6912]{1,0:T(8,128)(2,1)}, u32[]{:S(2)}, u32[]{:S(2)}) collective-permute-start(bf16[288,6912]{1,0:T(8,128)(2,1)} %copy.57), channel_id=1, source_target_pairs={{0,4},{4,0},{1,5},{5,1},{2,6},{6,2},{3,7},{7,3}} | collective-permute-start | bytes 11943944 | tf_op jit(solution)/shard_map/ppermute | solution.py:219
  19.5 89.2 %collective-permute-start.3 = (bf16[288,6912]{1,0:T(8,128)(2,1)}, bf16[288,6912]{1,0:T(8,128)(2,1)}, u32[]{:S(2)}, u32[]{:S(2)}) collective-permute-start(bf16[288,6912]{1,0:T(8,128)(2,1)} %copy.57), channel_id=1, source_target_pairs={{0,2},{1,3},{2,0},{3,1},{4,6},{5,7},{6,4},{7,5}} | collective-permute-start | bytes 11943944 | tf_op jit(solution)/shard_map/ppermute | solution.py:222
  21.0 96.8 %collective-permute-start.4 = (bf16[288,6912]{1,0:T(8,128)(2,1)}, bf16[288,6912]{1,0:T(8,128)(2,1)}, u32[]{:S(2)}, u32[]{:S(2)}) collective-permute-start(bf16[288,6912]{1,0:T(8,128)(2,1)} %copy.57), channel_id=1, source_target_pairs={{0,1},{1,0},{2,3},{3,2},{4,5},{5,4},{6,7},{7,6}} | collective-permute-start | bytes 11943944 | tf_op jit(solution)/shard_map/ppermute | solution.py:250
  22.6 290.9 %collective-permute-start = (bf16[288,2304]{1,0:T(8,128)(2,1)}, bf16[288,2304]{1,0:T(8,128)(2,1)}, u32[]{:S(2)}, u32[]{:S(2)}) collective-permute-start(bf16[288,2304]{1,0:T(8,128)(2,1)} %copy.53), channel_id=1, source_target_pairs={{0,4},{4,0},{1,5},{5,1},{2,6},{6,2},{3,7},{7,3}} | collective-permute-start | bytes 3981320 | tf_op jit(solution)/shard_map/ppermute | solution.py:219
  23.1 290.4 %collective-permute-start.1 = (bf16[288,2304]{1,0:T(8,128)(2,1)}, bf16[288,2304]{1,0:T(8,128)(2,1)}, u32[]{:S(2)}, u32[]{:S(2)}) collective-permute-start(bf16[288,2304]{1,0:T(8,128)(2,1)} %copy.53), channel_id=1, source_target_pairs={{0,2},{1,3},{2,0},{3,1},{4,6},{5,7},{6,4},{7,5}} | collective-permute-start | bytes 3981320 | tf_op jit(solution)/shard_map/ppermute | solution.py:222
  24.5 44.6 %copy-start.7 = (s32[4096]{0:T(1024)}, s32[4096]{0:T(1024)S(1)}, u32[]{:S(2)}) copy-start(s32[4096]{0:T(1024)S(1)} %eq.71) | copy-start | bytes 49156
  28.2 40.9 %copy-start.5 = (s32[4096]{0:T(1024)}, s32[4096]{0:T(1024)S(1)}, u32[]{:S(2)}) copy-start(s32[4096]{0:T(1024)S(1)} %fusion.11) | copy-start | bytes 49156
  28.9 23.2 %copy-start.14 = (s32[4096]{0:T(1024)}, s32[4096]{0:T(1024)S(1)}, u32[]{:S(2)}) copy-start(s32[4096]{0:T(1024)S(1)} %add_select_fusion.3) | copy-start | bytes 49156
  57.9 11.2 copy-start.2
  57.9 13.3 copy-start.15
  108.7 18.0 collective-permute-start.5
  108.7 112.3 %collective-permute-start.7 = (bf16[288,6912]{1,0:T(8,128)(2,1)}, bf16[288,6912]{1,0:T(8,128)(2,1)}, u32[]{:S(2)}, u32[]{:S(2)}) collective-permute-start(bf16[288,6912]{1,0:T(8,128)(2,1)} %collective-permute-done.2), channel_id=1, source_target_pairs={{0,2},{1,3},{2,0},{3,1},{4,6},{5,7},{6,4},{7,5}} | collective-permute-start | bytes 11943944 | tf_op jit(solution)/shard_map/ppermute | solution.py:222
  111.8 4.8 copy-start.4
  117.8 111.8 %collective-permute-start.6 = (bf16[288,6912]{1,0:T(8,128)(2,1)}, bf16[288,6912]{1,0:T(8,128)(2,1)S(1)}, u32[]{:S(2)}, u32[]{:S(2)}) collective-permute-start(bf16[288,6912]{1,0:T(8,128)(2,1)} %collective-permute-done.2), channel_id=1, source_target_pairs={{0,1},{1,0},{2,3},{3,2},{4,5},{5,4},{6,7},{7,6}} | collective-permute-start | bytes 11943944 | tf_op jit(solution)/shard_map/ppermute | solution.py:250
  126.6 270.0 %collective-permute-start.9 = (bf16[288,2304]{1,0:T(8,128)(2,1)}, bf16[288,2304]{1,0:T(8,128)(2,1)}, u32[]{:S(2)}, u32[]{:S(2)}) collective-permute-start(bf16[288,2304]{1,0:T(8,128)(2,1)} %copy.53), channel_id=1, source_target_pairs={{0,1},{1,0},{2,3},{3,2},{4,5},{5,4},{6,7},{7,6}} | collective-permute-start | bytes 3981320 | tf_op jit(solution)/shard_map/ppermute | solution.py:250
  221.0 15.7 collective-permute-start.8
  229.6 9.4 slice-start
  231.9 7.1 slice-start.1
  236.7 2.3 slice-start.2
  313.5 92.1 %collective-permute-start.11 = (bf16[288,2304]{1,0:T(8,128)(2,1)}, bf16[288,2304]{1,0:T(8,128)(2,1)S(1)}, u32[]{:S(2)}, u32[]{:S(2)}) collective-permute-start(bf16[288,2304]{1,0:T(8,128)(2,1)} %collective-permute-done), channel_id=1, source_target_pairs={{0,1},{1,0},{2,3},{3,2},{4,5},{5,4},{6,7},{7,6}} | collective-permute-start | bytes 3981320 | tf_op jit(solution)/shard_map/ppermute | solution.py:250
  314.1 87.5 %collective-permute-start.12 = (bf16[288,2304]{1,0:T(8,128)(2,1)}, bf16[288,2304]{1,0:T(8,128)(2,1)S(1)}, u32[]{:S(2)}, u32[]{:S(2)}) collective-permute-start(bf16[288,2304]{1,0:T(8,128)(2,1)} %collective-permute-done), channel_id=1, source_target_pairs={{0,2},{1,3},{2,0},{3,1},{4,6},{5,7},{6,4},{7,5}} | collective-permute-start | bytes 3981320 | tf_op jit(solution)/shard_map/ppermute | solution.py:222
  315.4 86.6 %collective-permute-start.10 = (bf16[288,2304]{1,0:T(8,128)(2,1)}, bf16[288,2304]{1,0:T(8,128)(2,1)S(1)}, u32[]{:S(2)}, u32[]{:S(2)}) collective-permute-start(bf16[288,2304]{1,0:T(8,128)(2,1)} %collective-permute-done.1), channel_id=1, source_target_pairs={{0,1},{1,0},{2,3},{3,2},{4,5},{5,4},{6,7},{7,6}} | collective-permute-start | bytes 3981320 | tf_op jit(solution)/shard_map/ppermute | solution.py:250
  392.8 3.7 copy-start.1
  401.6 6.4 collective-permute-start.13
  409.2 30.3 %copy-start.16 = (f32[2304]{0:T(1024)S(1)}, f32[2304]{0:T(1024)}, u32[]{:S(2)}) copy-start(f32[2304]{0:T(1024)} %param.16) | copy-start | bytes 27652
  439.5 10.0 copy-start.12
  449.2 528.5 %collective-permute-start.14 = (bf16[2048,2304]{1,0:T(8,128)(2,1)}, bf16[2048,2304]{1,0:T(8,128)(2,1)}, u32[]{:S(2)}, u32[]{:S(2)}) collective-permute-start(bf16[2048,2304]{1,0:T(8,128)(2,1)} %fusion.2), channel_id=1, source_target_pairs={{0,4},{4,0},{1,5},{5,1},{2,6},{6,2},{3,7},{7,3}} | collective-permute-start | bytes 28311560 | tf_op jit(solution)/shard_map/ppermute | solution.py:219
  477.0 528.1 %all-to-all-start.1 = ((bf16[4,640,2304]{2,1,0:T(8,128)(2,1)}), bf16[4,640,2304]{2,1,0:T(8,128)(2,1)}, u32[]{:S(2)}, u32[]{:S(2)}) async-start(bf16[4,640,2304]{2,1,0:T(8,128)(2,1)} %bitcast.121), calls=%async_computation.1 | async-start | bytes 23592960 | tf_op jit(solution)/shard_map/all_to_all | solution.py:239
  490.0 8.5 copy-start.8
  490.0 541.8 %collective-permute-start.18 = (bf16[1152,3072]{1,0:T(8,128)(2,1)}, bf16[1152,3072]{1,0:T(8,128)(2,1)}, u32[]{:S(2)}, u32[]{:S(2)}) collective-permute-start(bf16[1152,3072]{1,0:T(8,128)(2,1)} %dynamic-slice_bitcast_fusion.2), channel_id=1, source_target_pairs={{0,4},{4,0},{1,5},{5,1},{2,6},{6,2},{3,7},{7,3}} | collective-permute-start | bytes 21233672 | tf_op jit(solution)/shard_map/ppermute | solution.py:219
  498.2 533.9 %collective-permute-start.19 = (bf16[1152,3072]{1,0:T(8,128)(2,1)}, bf16[1152,3072]{1,0:T(8,128)(2,1)}, u32[]{:S(2)}, u32[]{:S(2)}) collective-permute-start(bf16[1152,3072]{1,0:T(8,128)(2,1)} %dynamic-slice_bitcast_fusion.1), channel_id=1, source_target_pairs={{0,4},{4,0},{1,5},{5,1},{2,6},{6,2},{3,7},{7,3}} | collective-permute-start | bytes 21233672 | tf_op jit(solution)/shard_map/ppermute | solution.py:219
  498.5 460.4 %collective-permute-start.15 = (s32[4096]{0:T(1024)S(1)}, s32[4096]{0:T(1024)S(1)}, u32[]{:S(2)}, u32[]{:S(2)}) collective-permute-start(s32[4096]{0:T(1024)S(1)} %copy-done.8), channel_id=1, source_target_pairs={{0,4},{4,0},{1,5},{5,1},{2,6},{6,2},{3,7},{7,3}} | collective-permute-start | bytes 49160 | tf_op jit(solution)/shard_map/ppermute | solution.py:219
  505.9 722.5 %collective-permute-start.16 = (bf16[1152,2688]{1,0:T(8,128)(2,1)}, bf16[1152,2688]{1,0:T(8,128)(2,1)}, u32[]{:S(2)}, u32[]{:S(2)}) collective-permute-start(bf16[1152,2688]{1,0:T(8,128)(2,1)} %dynamic-slice_bitcast_fusion.4), channel_id=1, source_target_pairs={{0,4},{4,0},{1,5},{5,1},{2,6},{6,2},{3,7},{7,3}} | collective-permute-start | bytes 18579464 | tf_op jit(solution)/shard_map/ppermute | solution.py:219
  1005.1 136.0 %all-to-all-start = ((bf16[4,640,2304]{2,1,0:T(8,128)(2,1)}), bf16[4,640,2304]{2,1,0:T(8,128)(2,1)}, u32[]{:S(2)}, u32[]{:S(2)}) async-start(bf16[4,640,2304]{2,1,0:T(8,128)(2,1)} %bitcast.122), calls=%async_computation | async-start | bytes 23592960 | tf_op jit(solution)/shard_map/all_to_all | solution.py:239
  1017.4 211.0 %collective-permute-start.17 = (bf16[1152,2688]{1,0:T(8,128)(2,1)}, bf16[1152,2688]{1,0:T(8,128)(2,1)}, u32[]{:S(2)}, u32[]{:S(2)}) collective-permute-start(bf16[1152,2688]{1,0:T(8,128)(2,1)} %dynamic-slice_bitcast_fusion.3), channel_id=1, source_target_pairs={{0,4},{4,0},{1,5},{5,1},{2,6},{6,2},{3,7},{7,3}} | collective-permute-start | bytes 18579464 | tf_op jit(solution)/shard_map/ppermute | solution.py:219
  1024.5 358.3 %collective-permute-start.20 = (bf16[5760,640]{1,0:T(8,128)(2,1)}, bf16[5760,640]{1,0:T(8,128)(2,1)}, u32[]{:S(2)}, u32[]{:S(2)}) collective-permute-start(bf16[5760,640]{1,0:T(8,128)(2,1)} %dynamic-slice_bitcast_fusion), channel_id=1, source_target_pairs={{0,4},{4,0},{1,5},{5,1},{2,6},{6,2},{3,7},{7,3}} | collective-permute-start | bytes 22118408 | tf_op jit(solution)/shard_map/ppermute | solution.py:219
  1031.8 476.2 %collective-permute-start.21 = (bf16[5760,512]{1,0:T(8,128)(2,1)}, bf16[5760,512]{1,0:T(8,128)(2,1)}, u32[]{:S(2)}, u32[]{:S(2)}) collective-permute-start(bf16[5760,512]{1,0:T(8,128)(2,1)} %dynamic-slice_bitcast_fusion.5), channel_id=1, source_target_pairs={{0,4},{4,0},{1,5},{5,1},{2,6},{6,2},{3,7},{7,3}} | collective-permute-start | bytes 17694728 | tf_op jit(solution)/shard_map/ppermute | solution.py:219
  1606.6 5.0 copy-start.6
  1606.6 7.0 copy-start.10
  1606.6 8.4 copy-start.13
  1606.6 9.4 copy-start.11
  1606.6 204.9 %all-to-all-start.2 = ((bf16[8,640,1792]{2,1,0:T(8,128)(2,1)}), bf16[8,640,1792]{2,1,0:T(8,128)(2,1)}, u32[]{:S(2)}, u32[]{:S(2)}) async-start(bf16[8,640,1792]{2,1,0:T(8,128)(2,1)} %bitcast.124), calls=%async_computation.2 | async-start | bytes 36700160 | tf_op jit(solution)/shard_map/all_to_all | solution.py:285
  1857.9 1.6 copy-start

commit v2 on v1

--- a/solution.py
+++ b/solution.py
@@ -94,16 +94,16 @@
 
 def up_kernel(ids_ref, z_a, z_b, wg_a, wg_b, wu_a, wu_b, *refs):
     mid_ref = refs[-1]
-    ff = mid_ref.shape[1]
+    ff = mid_ref.shape[2]
     w_a = jnp.concatenate([wg_a[0], wu_a[0]], axis=1)
     w_b = jnp.concatenate([wg_b[0], wu_b[0]], axis=1)
     w = jnp.concatenate([w_a, w_b], axis=0)
-    rows = mid_ref.shape[0]
+    rows = mid_ref.shape[0] * mid_ref.shape[1]
     start = pl.multiple_of(pl.program_id(1) * rows, rows)
     z = jnp.concatenate([z_a[pl.ds(start, rows), :], z_b[pl.ds(start, rows), :]], axis=1)
     acc = jnp.dot(z, w, preferred_element_type=jnp.float32)
     act_gate = acc[:, :ff]
-    mid_ref[...] = (act_gate * jax.nn.sigmoid(act_gate) * acc[:, ff:]).astype(mid_ref.dtype)
+    mid_ref[...] = (act_gate * jax.nn.sigmoid(act_gate) * acc[:, ff:]).astype(mid_ref.dtype).reshape(mid_ref.shape)
 
 
 def expert_up(ids, z, wg_own, wg_got, wu_own, wu_got, mid, first, ff, capacity, peer):
@@ -111,6 +111,8 @@
     half = model_dim // 2
     size, ff_dim = wg_got.shape[2], wg_own.shape[2]
     tiles, skip = size // ff, first // ff
+    devices = rows // capacity
+    pair = 2 if devices % 2 == 0 else 1
     own = pl.BlockSpec((1, half, ff), lambda j, i, s: (s[0], 0, skip + j))
     got = pl.BlockSpec((1, half, ff), lambda j, i, s: (0 if wg_got.shape[0] == 1 else 1 - s[0], 0, j))
     once = pl.Buffered(buffer_count=1)
@@ -119,15 +121,15 @@
         up_kernel,
         grid_spec=pltpu.PrefetchScalarGridSpec(
             num_scalar_prefetch=1,
-            grid=(tiles, rows // capacity),
+            grid=(tiles, devices // pair),
             in_specs=[
                 pl.BlockSpec((rows, half), lambda j, i, s: (0, s[0]), pipeline_mode=once),
                 pl.BlockSpec((rows, half), lambda j, i, s: (0, 1 - s[0]), pipeline_mode=once),
                 own, got, own, got,
             ] + [pl.BlockSpec(memory_space=pl.ANY)] * len(given),
-            out_specs=pl.BlockSpec((capacity, ff), lambda j, i, s: (2 * i + (1 - s[0] if peer else s[0]), skip + j)),
+            out_specs=pl.BlockSpec((pair, None, capacity, ff), lambda j, i, s: (i, 1 - s[0] if peer else s[0], 0, skip + j)),
         ),
-        out_shape=jax.ShapeDtypeStruct((2 * rows, ff_dim), jnp.bfloat16),
+        out_shape=jax.ShapeDtypeStruct((devices, 2, capacity, ff_dim), jnp.bfloat16),
         input_output_aliases={7: 0} if given else {},
         compiler_params=pltpu.CompilerParams(dimension_semantics=("arbitrary", "arbitrary"), vmem_limit_bytes=48 * 2**20),
         cost_estimate=pl.CostEstimate(flops=4 * rows * model_dim * size, bytes_accessed=2 * (rows * model_dim + 2 * model_dim * size + rows * size), transcendentals=rows * size),
@@ -251,7 +253,7 @@
             return whole.reshape(-1, part.shape[1]), first
 
         ff = tile_of(ff_dim, 384)
-        split = (ff_dim // ff + 1) // 2 * ff
+        split = ff_dim // ff * 3 // 5 * ff
         sends = [lax.dynamic_slice(p, (theirs, 0, first), (1, half, size))[0] for first, size in ((0, split), (split, ff_dim - split)) for p in (gate_part, up_part)]
         normed_x = rms_scale(x_loc, attn_gain).reshape(tok_dev, model_dim)
         out_t = out_part.reshape(num_heads * head_dim, -1).T
@@ -277,6 +279,8 @@
             for rows, peer in ((own_rows, False), (peer_rows, True)):
                 mid = expert_up(ids, rows, gate_part, wg_got, up_part, wu_got, mid, first, ff, capacity, peer)
 
+        mid = mid.reshape(num_experts * capacity, ff_dim)
+
         once = pl.Buffered(buffer_count=1)
         spec_own = pl.BlockSpec((1, ff_dim, half), lambda i, s: (s[0], 0, 0), pipeline_mode=once)
         spec_got = [pl.BlockSpec(part.shape, lambda i, s: (0, 0), pipeline_mode=once) for part in got_down]

time: 1880 us -> 1900 us (1.011)
  waiting for transfers between devices: 770 us -> 797 us
    ppermute x10, waiting for transfers between devices: 483 us -> 511 us  [swap(): return lax.ppermute(value, 'data', other_data)]
  transfers between devices with their start and end apart: 25 -> 25, of which waited for: 7 -> 6; matrix products, arithmetic and copies ran while one was open for 17% -> 17% of each run, Pallas kernels for 28% -> 27%
where the time goes in v2:
time: 1900 us; the launch traced here: 1890 us
  waiting for transfers between devices  797 us (42%)
  Pallas kernels  568 us (30%)
  local copies, waits for them, and re-layouts  291 us (15%)
  matrix products  105 us (6%)
  blocking collectives  61.4 us (3%)
  starting transfers between devices  34.3 us (2%)
  other arithmetic  34 us (2%)
    ppermute x10, waiting for transfers between devices, swap(): return lax.ppermute(value, 'data', other_data)  511 us
    pallas_call x4, Pallas kernels, expert_up(): pl.pallas_call(up_kernel, grid_spec=pltpu.PrefetchScalarGridSpec(num_scal...  317 us
    all_to_all x1, waiting for transfers between devices, back(): lax.all_to_all(cols.reshape(num_experts, capacity, -1), token_axes, 0, 0,...  169 us
    pallas_call x2, Pallas kernels, expert_down(): pl.pallas_call(down_kernel, grid_spec=pltpu.PrefetchScalarGridSpec(num_sc...  158 us
    ppermute x4, waiting for transfers between devices, cross(): return lax.ppermute(value, 'expert', other_chip)  96.2 us
    pallas_call x1, Pallas kernels, attention_core(): pl.pallas_call(functools.partial(attention_kernel, head_dim, num_heads),...  77.4 us
    dot_general x1, matrix products, local_step(): jnp.dot(normed_x, w_qkv, preferred_element_type=jnp.float32)  74.6 us
    gather x4, local copies, waits for them, and re-layouts, local_step(): p.at[pick[:, k]].get(mode='promise_in_bounds')  69.6 us
  transfers between devices with their start and end apart: 25, of which 6 were waited for; matrix products, arithmetic and copies ran while one was open for 17% of the time, Pallas kernels for 27%

profile of v2, /device:TPU:0, one launch (start us, length us, event | category | flops | bytes accessed | tf_op | source)
XLA Modules:
  0.0 1890.4 jit_solution(10156189780296443811)
XLA Ops:
  0.0 9.4 copy.56
  9.4 6.7 copy.57
  16.1 3.3 collective-permute-start.2
  28.9 6.7 copy.60
  35.6 16.5 scatter_custom_fusion
  52.2 5.6 multiply_reduce_fusion
  57.9 11.2 broadcast_in_dim.100
  71.3 9.6 multiply_convert_fusion
  80.9 25.7 %collective-permute-done.2 = bf16[288,6912]{1,0:T(8,128)(2,1)} collective-permute-done((bf16[288,6912]{1,0:T(8,128)(2,1)}, bf16[288,6912]{1,0:T(8,128)(2,1)}, u32[]{:S(2)}, u32[]{:S(2)}) %collective-permute-start.2) | collective-permute-done | bytes 3981344 | tf_op jit(solution)/shard_map/ppermute | solution.py:221
  112.0 4.6 broadcast_in_dim.98
  118.0 4.3 bitcast_dynamic-update-slice_fusion.6
  122.3 4.3 bitcast_dynamic-update-slice_fusion.5
  126.8 94.2 %collective-permute-done.7 = bf16[288,6912]{1,0:T(8,128)(2,1)} collective-permute-done((bf16[288,6912]{1,0:T(8,128)(2,1)}, bf16[288,6912]{1,0:T(8,128)(2,1)}, u32[]{:S(2)}, u32[]{:S(2)}) %collective-permute-start.7) | collective-permute-done | bytes 3981344 | tf_op jit(solution)/shard_map/ppermute | solution.py:224
  221.0 4.3 bitcast_dynamic-update-slice_fusion.4
  225.3 4.3 bitcast_dynamic-update-slice_fusion.3
  231.9 4.8 bitcast_dynamic-update-slice_fusion.1
  238.9 74.6 %convolution_convert_fusion.qkv_ref = bf16[2048,6912]{1,0:T(8,128)(2,1)} fusion(bf16[2048,2304]{1,0:T(8,128)(2,1)S(1)} %bitcast.130, bf16[2304,6912]{1,0:T(8,128)(2,1)} %bitcast.126), kind=kOutput, calls=%fused_computation.8 | convolution fusion | flops 65243971584 | bytes 69599232 | tf_op jit(solution)/shard_map/dot_general | solution.py:267
  315.4 77.4 %attention_core.1 = bf16[2048,2304]{1,0:T(8,128)(2,1)S(1)} custom-call(bf16[2048,6912]{1,0:T(8,128)(2,1)} %convolution_convert_fusion.qkv_ref, f32[128,128]{1,0:T(8,128)S(1)} %copy.65.cos_ref, f32[128,128]{1,0:T(8,128)S(1)} %copy.66.sin_ref), custom_call_target="tpu_custom_call" | custom-call | flops 40000000000 | bytes 37748736 | tf_op jit(solution)/shard_map/attention_core/pallas_call | solution.py:69
  392.9 3.7 copy-done.1
  409.2 30.3 %fusion = (f32[2048]{0:T(1024)S(1)}, bf16[2048,2304]{1,0:T(8,128)(2,1)}) fusion(bf16[2048,2304]{1,0:T(8,128)(2,1)} %copy-done.1, bf16[2304,2304]{1,0:T(8,128)(2,1)} %bitcast.27, bf16[16,128,2304]{2,1,0:T(8,128)(2,1)} %param.10), kind=kOutput, calls=%fused_computation.11 | convolution fusion | flops 21771581440 | bytes 38936576 | tf_op jit(solution)/shard_map/dot_general | solution.py:270
  439.5 9.6 fusion.2
  449.5 27.5 %gather_fusion.1 = bf16[2560,2304]{1,0:T(8,128)(2,1)} fusion(bf16[2048,2304]{1,0:T(8,128)(2,1)} %fusion.2, s32[3072]{0:T(1024)S(1)} %pad_clamp_fusion), kind=kCustom, calls=%fused_computation.1 | custom fusion | bytes 23603200 | tf_op jit(solution)/shard_map/gather | solution.py:240
  477.0 6.6 all-to-all-start.1
  483.6 6.9 dynamic-slice_bitcast_fusion.1
  492.2 7.0 dynamic-slice_bitcast_fusion
  501.2 5.1 dynamic-slice_bitcast_fusion.5
  506.7 5.2 dynamic-slice_bitcast_fusion.4
  511.9 484.9 %collective-permute-done.15 = s32[4096]{0:T(1024)S(1)} collective-permute-done((s32[4096]{0:T(1024)S(1)}, s32[4096]{0:T(1024)S(1)}, u32[]{:S(2)}, u32[]{:S(2)}) %collective-permute-start.15) | collective-permute-done | bytes 16416 | tf_op jit(solution)/shard_map/ppermute | solution.py:221
  1000.3 15.7 scatter_custom_fusion.1
  1016.0 27.4 %gather_fusion = bf16[2560,2304]{1,0:T(8,128)(2,1)} fusion(bf16[2048,2304]{1,0:T(8,128)(2,1)} %collective-permute-done.14, s32[3072]{0:T(1024)S(1)} %pad_clamp_fusion.1), kind=kCustom, calls=%fused_computation | custom fusion | bytes 23603200 | tf_op jit(solution)/shard_map/gather | solution.py:240
  1043.4 6.4 all-to-all-start
  1049.8 6.8 dynamic-slice_bitcast_fusion.2
  1058.3 5.6 dynamic-slice_bitcast_fusion.3
  1064.2 93.6 %expert_up.4.refs_0_ = bf16[4,2,640,5760]{3,2,1,0:T(8,128)(2,1)} custom-call(s32[1]{0:T(128)} %bitcast.28.ids_ref, bf16[2560,2304]{1,0:T(8,128)(2,1)} %bitcast.38.z_a.z_b, bf16[2560,2304]{1,0:T(8,128)(2,1)} %bitcast.38.z_a.z_b, bf16[2,1152,5760]{2,1,0:T(8,128)(2,1)} %wg_a.7, bf16[1,1152,3456]{2,1,0:T(8,128)(2,1)} %bitcast.40.wg_b, ...), custom_call_target="tpu_custom_call" | custom-call | flops 81537269760 | bytes 61341696 | tf_op jit(solution)/shard_map/expert_up/pallas_call | solution.py:120
  1157.9 21.6 %all-to-all-done = bf16[4,640,2304]{2,1,0:T(8,128)(2,1)} async-done(((bf16[4,640,2304]{2,1,0:T(8,128)(2,1)}), bf16[4,640,2304]{2,1,0:T(8,128)(2,1)}, u32[]{:S(2)}, u32[]{:S(2)}) %all-to-all-start) | async-done | bytes 11796512 | tf_op jit(solution)/shard_map/all_to_all | solution.py:241
  1179.5 93.6 %expert_up.5.refs_0_ = bf16[4,2,640,5760]{3,2,1,0:T(8,128)(2,1)} custom-call(s32[1]{0:T(128)} %bitcast.28.ids_ref, bf16[2560,2304]{1,0:T(8,128)(2,1)} %bitcast.32.z_a.z_b, bf16[2560,2304]{1,0:T(8,128)(2,1)} %bitcast.32.z_a.z_b, bf16[2,1152,5760]{2,1,0:T(8,128)(2,1)} %wg_a.7, bf16[1,1152,3456]{2,1,0:T(8,128)(2,1)} %bitcast.40.wg_b, ...), custom_call_target="tpu_custom_call", output_to_operand_aliasing={{}: (7, {})} | custom-call | flops 81537269760 | bytes 61341696 | tf_op jit(solution)/shard_map/expert_up/pallas_call | solution.py:120
  1273.1 64.6 %expert_up.6.refs_0_ = bf16[4,2,640,5760]{3,2,1,0:T(8,128)(2,1)} custom-call(s32[1]{0:T(128)} %bitcast.28.ids_ref, bf16[2560,2304]{1,0:T(8,128)(2,1)} %bitcast.38.z_a.z_b, bf16[2560,2304]{1,0:T(8,128)(2,1)} %bitcast.38.z_a.z_b, bf16[2,1152,5760]{2,1,0:T(8,128)(2,1)} %wg_a.7, bf16[1,1152,2304]{2,1,0:T(8,128)(2,1)} %bitcast.34.wg_b, ...), custom_call_target="tpu_custom_call", output_to_operand_aliasing={{}: (7, {})} | custom-call | flops 54358179840 | bytes 44826624 | tf_op jit(solution)/shard_map/expert_up/pallas_call | solution.py:120
  1337.7 65.0 %expert_up.7 = bf16[4,2,640,5760]{3,2,1,0:T(8,128)(2,1)} custom-call(s32[1]{0:T(128)} %bitcast.28.ids_ref, bf16[2560,2304]{1,0:T(8,128)(2,1)} %bitcast.32.z_a.z_b, bf16[2560,2304]{1,0:T(8,128)(2,1)} %bitcast.32.z_a.z_b, bf16[2,1152,5760]{2,1,0:T(8,128)(2,1)} %wg_a.7, bf16[1,1152,2304]{2,1,0:T(8,128)(2,1)} %bitcast.34.wg_b, ...), custom_call_target="tpu_custom_call", output_to_operand_aliasing={{}: (7, {})} | custom-call | flops 54358179840 | bytes 44826624 | tf_op jit(solution)/shard_map/expert_up/pallas_call | solution.py:120
  1402.7 120.4 %shard_map.100 = bf16[5120,1792]{1,0:T(8,128)(2,1)} custom-call(s32[1]{0:T(128)} %bitcast.28.ids_ref, bf16[5120,5760]{1,0:T(8,128)(2,1)} %bitcast.120, bf16[2,5760,1152]{2,1,0:T(8,128)(2,1)} %refs_0_.1, bf16[5760,640]{1,0:T(8,128)(2,1)} %collective-permute-done.20.refs_1_), custom_call_target="tpu_custom_call" | custom-call | flops 105696460800 | bytes 97976320 | tf_op jit(solution)/shard_map/pallas_call | solution.py:150
  1523.1 37.2 %shard_map.101 = bf16[5120,512]{1,0:T(8,128)(2,1)S(1)} custom-call(s32[1]{0:T(128)} %bitcast.28.ids_ref, bf16[5120,5760]{1,0:T(8,128)(2,1)} %bitcast.121, bf16[5760,512]{1,0:T(8,128)(2,1)} %collective-permute-done.21.refs_0_), custom_call_target="tpu_custom_call" | custom-call | flops 30198988800 | bytes 70123520 | tf_op jit(solution)/shard_map/pallas_call | solution.py:150
  1560.3 61.4 %all_to_all.20 = bf16[8,640,512]{2,1,0:T(8,128)(2,1)} all-to-all(bf16[8,640,512]{2,1,0:T(8,128)(2,1)S(1)} %bitcast.117), channel_id=1, replica_groups=mesh['rep'=1,'data'=2,'expert'=4] {'expert','data'}, dimensions={0} | all-to-all | bytes 10485760 | tf_op jit(solution)/shard_map/all_to_all | solution.py:289
  1621.7 4.9 all-to-all-start.2
  1634.7 10.8 gather_fusion.5
  1645.5 12.4 gather_fusion.3
  1657.9 168.7 %all-to-all-done.2 = bf16[8,640,1792]{2,1,0:T(8,128)(2,1)} async-done(((bf16[8,640,1792]{2,1,0:T(8,128)(2,1)}), bf16[8,640,1792]{2,1,0:T(8,128)(2,1)}, u32[]{:S(2)}, u32[]{:S(2)}) %all-to-all-start.2) | async-done | bytes 18350112 | tf_op jit(solution)/shard_map/all_to_all | solution.py:289
  1826.6 23.2 %gather_fusion.4 = bf16[2048,1792]{1,0:T(8,128)(2,1)} fusion(bf16[5120,1792]{1,0:T(8,128)(2,1)} %bitcast.47, s32[2048]{0:T(1024)S(1)} %get-tuple-element.42), kind=kCustom, calls=%fused_computation.4 | custom fusion | bytes 14688256 | tf_op jit(solution)/shard_map/gather | solution.py:300
  1849.7 23.2 %gather_fusion.2 = bf16[2048,1792]{1,0:T(8,128)(2,1)} fusion(bf16[5120,1792]{1,0:T(8,128)(2,1)} %bitcast.47, s32[2048]{0:T(1024)S(1)} %get-tuple-element.43), kind=kCustom, calls=%fused_computation.2 | custom fusion | bytes 14688256 | tf_op jit(solution)/shard_map/gather | solution.py:300
  1874.5 15.7 combine.1
  (138 shorter events, 57.2 us)
Async XLA Ops:
  0.0 21.0 %copy-start.3 = (bf16[36,64,288]{2,1,0:T(8,128)(2,1)S(1)}, bf16[36,64,288]{2,1,0:T(8,128)(2,1)}, u32[]{:S(2)}) copy-start(bf16[36,64,288]{2,1,0:T(8,128)(2,1)} %param.15) | copy-start | bytes 3981316
  0.0 23.1 %copy-start.9 = (s32[16,128,2]{1,2,0:T(2,128)S(1)}, s32[16,128,2]{1,2,0:T(2,128)}, u32[]{:S(2)}) copy-start(s32[16,128,2]{1,2,0:T(2,128)} %param.11) | copy-start | bytes 49156
  16.1 90.5 %collective-permute-start.2 = (bf16[288,6912]{1,0:T(8,128)(2,1)}, bf16[288,6912]{1,0:T(8,128)(2,1)}, u32[]{:S(2)}, u32[]{:S(2)}) collective-permute-start(bf16[288,6912]{1,0:T(8,128)(2,1)} %copy.57), channel_id=1, source_target_pairs={{0,4},{4,0},{1,5},{5,1},{2,6},{6,2},{3,7},{7,3}} | collective-permute-start | bytes 11943944 | tf_op jit(solution)/shard_map/ppermute | solution.py:221
  19.5 89.2 %collective-permute-start.3 = (bf16[288,6912]{1,0:T(8,128)(2,1)}, bf16[288,6912]{1,0:T(8,128)(2,1)}, u32[]{:S(2)}, u32[]{:S(2)}) collective-permute-start(bf16[288,6912]{1,0:T(8,128)(2,1)} %copy.57), channel_id=1, source_target_pairs={{0,2},{1,3},{2,0},{3,1},{4,6},{5,7},{6,4},{7,5}} | collective-permute-start | bytes 11943944 | tf_op jit(solution)/shard_map/ppermute | solution.py:224
  21.0 96.8 %collective-permute-start.4 = (bf16[288,6912]{1,0:T(8,128)(2,1)}, bf16[288,6912]{1,0:T(8,128)(2,1)}, u32[]{:S(2)}, u32[]{:S(2)}) collective-permute-start(bf16[288,6912]{1,0:T(8,128)(2,1)} %copy.57), channel_id=1, source_target_pairs={{0,1},{1,0},{2,3},{3,2},{4,5},{5,4},{6,7},{7,6}} | collective-permute-start | bytes 11943944 | tf_op jit(solution)/shard_map/ppermute | solution.py:252
  22.6 290.9 %collective-permute-start = (bf16[288,2304]{1,0:T(8,128)(2,1)}, bf16[288,2304]{1,0:T(8,128)(2,1)}, u32[]{:S(2)}, u32[]{:S(2)}) collective-permute-start(bf16[288,2304]{1,0:T(8,128)(2,1)} %copy.53), channel_id=1, source_target_pairs={{0,4},{4,0},{1,5},{5,1},{2,6},{6,2},{3,7},{7,3}} | collective-permute-start | bytes 3981320 | tf_op jit(solution)/shard_map/ppermute | solution.py:221
  23.1 290.4 %collective-permute-start.1 = (bf16[288,2304]{1,0:T(8,128)(2,1)}, bf16[288,2304]{1,0:T(8,128)(2,1)}, u32[]{:S(2)}, u32[]{:S(2)}) collective-permute-start(bf16[288,2304]{1,0:T(8,128)(2,1)} %copy.53), channel_id=1, source_target_pairs={{0,2},{1,3},{2,0},{3,1},{4,6},{5,7},{6,4},{7,5}} | collective-permute-start | bytes 3981320 | tf_op jit(solution)/shard_map/ppermute | solution.py:224
  24.5 44.6 %copy-start.7 = (s32[4096]{0:T(1024)}, s32[4096]{0:T(1024)S(1)}, u32[]{:S(2)}) copy-start(s32[4096]{0:T(1024)S(1)} %eq.71) | copy-start | bytes 49156
  28.2 40.9 %copy-start.5 = (s32[4096]{0:T(1024)}, s32[4096]{0:T(1024)S(1)}, u32[]{:S(2)}) copy-start(s32[4096]{0:T(1024)S(1)} %fusion.11) | copy-start | bytes 49156
  28.9 23.2 %copy-start.14 = (s32[4096]{0:T(1024)}, s32[4096]{0:T(1024)S(1)}, u32[]{:S(2)}) copy-start(s32[4096]{0:T(1024)S(1)} %add_select_fusion.3) | copy-start | bytes 49156
  57.9 11.2 copy-start.2
  57.9 13.3 copy-start.15
  108.7 18.0 collective-permute-start.5
  108.7 112.3 %collective-permute-start.7 = (bf16[288,6912]{1,0:T(8,128)(2,1)}, bf16[288,6912]{1,0:T(8,128)(2,1)}, u32[]{:S(2)}, u32[]{:S(2)}) collective-permute-start(bf16[288,6912]{1,0:T(8,128)(2,1)} %collective-permute-done.2), channel_id=1, source_target_pairs={{0,2},{1,3},{2,0},{3,1},{4,6},{5,7},{6,4},{7,5}} | collective-permute-start | bytes 11943944 | tf_op jit(solution)/shard_map/ppermute | solution.py:224
  111.8 4.8 copy-start.4
  117.8 111.8 %collective-permute-start.6 = (bf16[288,6912]{1,0:T(8,128)(2,1)}, bf16[288,6912]{1,0:T(8,128)(2,1)S(1)}, u32[]{:S(2)}, u32[]{:S(2)}) collective-permute-start(bf16[288,6912]{1,0:T(8,128)(2,1)} %collective-permute-done.2), channel_id=1, source_target_pairs={{0,1},{1,0},{2,3},{3,2},{4,5},{5,4},{6,7},{7,6}} | collective-permute-start | bytes 11943944 | tf_op jit(solution)/shard_map/ppermute | solution.py:252
  126.6 270.0 %collective-permute-start.9 = (bf16[288,2304]{1,0:T(8,128)(2,1)}, bf16[288,2304]{1,0:T(8,128)(2,1)}, u32[]{:S(2)}, u32[]{:S(2)}) collective-permute-start(bf16[288,2304]{1,0:T(8,128)(2,1)} %copy.53), channel_id=1, source_target_pairs={{0,1},{1,0},{2,3},{3,2},{4,5},{5,4},{6,7},{7,6}} | collective-permute-start | bytes 3981320 | tf_op jit(solution)/shard_map/ppermute | solution.py:252
  221.0 15.7 collective-permute-start.8
  229.6 9.4 slice-start
  231.9 7.1 slice-start.1
  236.7 2.3 slice-start.2
  313.5 92.1 %collective-permute-start.11 = (bf16[288,2304]{1,0:T(8,128)(2,1)}, bf16[288,2304]{1,0:T(8,128)(2,1)S(1)}, u32[]{:S(2)}, u32[]{:S(2)}) collective-permute-start(bf16[288,2304]{1,0:T(8,128)(2,1)} %collective-permute-done), channel_id=1, source_target_pairs={{0,1},{1,0},{2,3},{3,2},{4,5},{5,4},{6,7},{7,6}} | collective-permute-start | bytes 3981320 | tf_op jit(solution)/shard_map/ppermute | solution.py:252
  314.1 87.5 %collective-permute-start.12 = (bf16[288,2304]{1,0:T(8,128)(2,1)}, bf16[288,2304]{1,0:T(8,128)(2,1)S(1)}, u32[]{:S(2)}, u32[]{:S(2)}) collective-permute-start(bf16[288,2304]{1,0:T(8,128)(2,1)} %collective-permute-done), channel_id=1, source_target_pairs={{0,2},{1,3},{2,0},{3,1},{4,6},{5,7},{6,4},{7,5}} | collective-permute-start | bytes 3981320 | tf_op jit(solution)/shard_map/ppermute | solution.py:224
  315.4 86.6 %collective-permute-start.10 = (bf16[288,2304]{1,0:T(8,128)(2,1)}, bf16[288,2304]{1,0:T(8,128)(2,1)S(1)}, u32[]{:S(2)}, u32[]{:S(2)}) collective-permute-start(bf16[288,2304]{1,0:T(8,128)(2,1)} %collective-permute-done.1), channel_id=1, source_target_pairs={{0,1},{1,0},{2,3},{3,2},{4,5},{5,4},{6,7},{7,6}} | collective-permute-start | bytes 3981320 | tf_op jit(solution)/shard_map/ppermute | solution.py:252
  392.8 3.7 copy-start.1
  401.6 6.4 collective-permute-start.13
  409.2 30.3 %copy-start.16 = (f32[2304]{0:T(1024)S(1)}, f32[2304]{0:T(1024)}, u32[]{:S(2)}) copy-start(f32[2304]{0:T(1024)} %param.16) | copy-start | bytes 27652
  439.5 10.0 copy-start.12
  449.2 566.8 %collective-permute-start.14 = (bf16[2048,2304]{1,0:T(8,128)(2,1)}, bf16[2048,2304]{1,0:T(8,128)(2,1)}, u32[]{:S(2)}, u32[]{:S(2)}) collective-permute-start(bf16[2048,2304]{1,0:T(8,128)(2,1)} %fusion.2), channel_id=1, source_target_pairs={{0,4},{4,0},{1,5},{5,1},{2,6},{6,2},{3,7},{7,3}} | collective-permute-start | bytes 28311560 | tf_op jit(solution)/shard_map/ppermute | solution.py:221
  477.0 566.4 %all-to-all-start.1 = ((bf16[4,640,2304]{2,1,0:T(8,128)(2,1)}), bf16[4,640,2304]{2,1,0:T(8,128)(2,1)}, u32[]{:S(2)}, u32[]{:S(2)}) async-start(bf16[4,640,2304]{2,1,0:T(8,128)(2,1)} %bitcast.124), calls=%async_computation.1 | async-start | bytes 23592960 | tf_op jit(solution)/shard_map/all_to_all | solution.py:241
  490.5 9.1 copy-start.8
  490.5 573.4 %collective-permute-start.18 = (bf16[1152,3456]{1,0:T(8,128)(2,1)}, bf16[1152,3456]{1,0:T(8,128)(2,1)}, u32[]{:S(2)}, u32[]{:S(2)}) collective-permute-start(bf16[1152,3456]{1,0:T(8,128)(2,1)} %dynamic-slice_bitcast_fusion.1), channel_id=1, source_target_pairs={{0,4},{4,0},{1,5},{5,1},{2,6},{6,2},{3,7},{7,3}} | collective-permute-start | bytes 23887880 | tf_op jit(solution)/shard_map/ppermute | solution.py:221
  499.2 565.0 %collective-permute-start.19 = (bf16[1152,3456]{1,0:T(8,128)(2,1)}, bf16[1152,3456]{1,0:T(8,128)(2,1)}, u32[]{:S(2)}, u32[]{:S(2)}) collective-permute-start(bf16[1152,3456]{1,0:T(8,128)(2,1)} %dynamic-slice_bitcast_fusion), channel_id=1, source_target_pairs={{0,4},{4,0},{1,5},{5,1},{2,6},{6,2},{3,7},{7,3}} | collective-permute-start | bytes 23887880 | tf_op jit(solution)/shard_map/ppermute | solution.py:221
  499.6 497.2 %collective-permute-start.15 = (s32[4096]{0:T(1024)S(1)}, s32[4096]{0:T(1024)S(1)}, u32[]{:S(2)}, u32[]{:S(2)}) collective-permute-start(s32[4096]{0:T(1024)S(1)} %copy-done.8), channel_id=1, source_target_pairs={{0,4},{4,0},{1,5},{5,1},{2,6},{6,2},{3,7},{7,3}} | collective-permute-start | bytes 49160 | tf_op jit(solution)/shard_map/ppermute | solution.py:221
  506.4 766.7 %collective-permute-start.16 = (bf16[1152,2304]{1,0:T(8,128)(2,1)}, bf16[1152,2304]{1,0:T(8,128)(2,1)}, u32[]{:S(2)}, u32[]{:S(2)}) collective-permute-start(bf16[1152,2304]{1,0:T(8,128)(2,1)} %dynamic-slice_bitcast_fusion.5), channel_id=1, source_target_pairs={{0,4},{4,0},{1,5},{5,1},{2,6},{6,2},{3,7},{7,3}} | collective-permute-start | bytes 15925256 | tf_op jit(solution)/shard_map/ppermute | solution.py:221
  996.8 276.3 %collective-permute-start.17 = (bf16[1152,2304]{1,0:T(8,128)(2,1)}, bf16[1152,2304]{1,0:T(8,128)(2,1)}, u32[]{:S(2)}, u32[]{:S(2)}) collective-permute-start(bf16[1152,2304]{1,0:T(8,128)(2,1)} %dynamic-slice_bitcast_fusion.4), channel_id=1, source_target_pairs={{0,4},{4,0},{1,5},{5,1},{2,6},{6,2},{3,7},{7,3}} | collective-permute-start | bytes 15925256 | tf_op jit(solution)/shard_map/ppermute | solution.py:221
  1043.4 136.0 %all-to-all-start = ((bf16[4,640,2304]{2,1,0:T(8,128)(2,1)}), bf16[4,640,2304]{2,1,0:T(8,128)(2,1)}, u32[]{:S(2)}, u32[]{:S(2)}) async-start(bf16[4,640,2304]{2,1,0:T(8,128)(2,1)} %bitcast.125), calls=%async_computation | async-start | bytes 23592960 | tf_op jit(solution)/shard_map/all_to_all | solution.py:241
  1056.6 346.1 %collective-permute-start.20 = (bf16[5760,640]{1,0:T(8,128)(2,1)}, bf16[5760,640]{1,0:T(8,128)(2,1)}, u32[]{:S(2)}, u32[]{:S(2)}) collective-permute-start(bf16[5760,640]{1,0:T(8,128)(2,1)} %dynamic-slice_bitcast_fusion.2), channel_id=1, source_target_pairs={{0,4},{4,0},{1,5},{5,1},{2,6},{6,2},{3,7},{7,3}} | collective-permute-start | bytes 22118408 | tf_op jit(solution)/shard_map/ppermute | solution.py:221
  1063.9 459.2 %collective-permute-start.21 = (bf16[5760,512]{1,0:T(8,128)(2,1)}, bf16[5760,512]{1,0:T(8,128)(2,1)}, u32[]{:S(2)}, u32[]{:S(2)}) collective-permute-start(bf16[5760,512]{1,0:T(8,128)(2,1)} %dynamic-slice_bitcast_fusion.3), channel_id=1, source_target_pairs={{0,4},{4,0},{1,5},{5,1},{2,6},{6,2},{3,7},{7,3}} | collective-permute-start | bytes 17694728 | tf_op jit(solution)/shard_map/ppermute | solution.py:221
  1621.7 4.9 copy-start.6
  1621.7 6.9 copy-start.10
  1621.7 8.3 copy-start.13
  1621.7 9.3 copy-start.11
  1621.7 204.8 %all-to-all-start.2 = ((bf16[8,640,1792]{2,1,0:T(8,128)(2,1)}), bf16[8,640,1792]{2,1,0:T(8,128)(2,1)}, u32[]{:S(2)}, u32[]{:S(2)}) async-start(bf16[8,640,1792]{2,1,0:T(8,128)(2,1)} %bitcast.127), calls=%async_computation.2 | async-start | bytes 36700160 | tf_op jit(solution)/shard_map/all_to_all | solution.py:289
  1872.9 1.6 copy-start
